TPU v7x, 256 devices: a whole 4x4x8 slice. The times are simulated.
256 devices in a mesh: pair: 32 (over z, y), aux: 8 (over x, core).
Axes of the slice: x: 4, y: 4, z: 8, core: 2. Of those that a mesh axis runs over, the one named last changes fastest.
Arguments:
- ints_ac: bfloat16 [768, 512, 4096], P(None, ('pair', 'aux')), may hold values from -0.375 to 0.375
- slot_pair: int32 [768], replicated, may hold values from 0 to 767, each once
- amplitudes: bfloat16 [768, 2, 4096], P(('pair', 'aux')), may hold values from -6 to 6
- ranks: int32 [768], P(('pair', 'aux')), may hold values from 16 to 64
- pair_occ: int32 [768, 2], P(('pair', 'aux')), may hold values from 0 to 47
- pno_energy: float32 [768, 64], P(('pair', 'aux')), may hold values from 0.2 to 3
- occ_energy: float32 [48], replicated, may hold values from -2 to -0.3
Outputs:
- ext_residual: float32 [768, 2, 4096], P(('pair', 'aux'))
- new_amplitudes: bfloat16 [768, 2, 4096], P(('pair', 'aux'))
Inputs may be any that keep to these rules, and one draw needn't show every extreme that they name: `slot_pair`: a permutation of the pairs. Entries a >= ranks[s] of a slot's blocks are padding.
All inputs are finite; a program needn't handle non-finite values.
Results may differ from a plain program's by a relative error of at most 0.0039.
Values may be sent and summed in bfloat16 or wider, within the bound.
No kernel may reach another device: no remote copies, remote signals or barrier semaphores. Data moves between devices by JAX's collectives and lax.ppermute only.
A program may use at most 128 MiB of HBM per device.

v0:
```python
import jax
import jax.numpy as jnp
from jax import lax
from jax.experimental import pallas as pl
from jax.experimental.pallas import tpu as pltpu
from jax.sharding import Mesh, PartitionSpec as P


SIDES = (4, 4, 2)
AXES = ("z", "y", "x", "core")
BF16, F32 = jnp.bfloat16, jnp.float32


def moved(value, axis, step):
    n = lax.axis_size(axis)
    return lax.ppermute(value, axis, [(j, (j + step) % n) for j in range(n)])


class Plan:
    def __init__(self, sizes, local):
        self.nz, self.ny, self.nx, self.nc = sizes
        assert self.ny == self.nx
        self.ring = self.nx
        self.local = local
        self.half = self.nz // 2
        self.batch = self.half * local
        self.rows = 2 * self.ring

    def slot(self, s, g, n, meta, core):
        h, t = g // self.ring, g % self.ring
        sy = jnp.where(h == 0, s, t)
        sx = jnp.where(h == 0, t, s)
        y = lax.rem(meta[1] - sy + self.ring, self.ring)
        x = lax.rem(meta[2] - sx + self.ring, self.ring)
        z = n // self.local + h * self.half
        return (((z * self.ny + y) * self.nx + x) * self.nc + core) * self.local + n % self.local


def collect(plan, rows, slot_pair, meta):
    width, lanes = rows.shape[1:]
    batch = plan.batch
    steps = plan.ring * plan.rows

    def kernel(sp, where, *refs):
        out = refs[-1]
        for n in range(batch):
            out[n] = refs[n][0]

    def spec(n):
        def where_is(g, sp, where):
            return sp[plan.slot(g // plan.rows, g % plan.rows, n, where, 1 - where[3])], 0, 0

        return pl.BlockSpec((1, width, lanes), where_is)

    return pl.pallas_call(
        kernel,
        grid_spec=pltpu.PrefetchScalarGridSpec(
            num_scalar_prefetch=2,
            grid=(steps,),
            in_specs=[spec(n) for n in range(batch)],
            out_specs=pl.BlockSpec((batch, width, lanes), lambda g, sp, where: (g, 0, 0)),
        ),
        out_shape=jax.ShapeDtypeStruct((steps * batch, width, lanes), rows.dtype),
        cost_estimate=pl.CostEstimate(
            flops=steps * batch * 10**6, bytes_accessed=steps * batch * 32768, transcendentals=0
        ),
        name="collect",
    )(slot_pair, meta, *([rows] * batch))


def assemble(plan, column, parts):
    batch, ring = plan.batch, plan.ring
    tail = column.shape[1:]

    def kernel(own, *refs):
        got, outs = refs[:-2], refs[-2:]
        for h in range(2):
            outs[h][pl.ds(0, batch)] = own[pl.ds(h * batch, batch)]
            for t in range(1, ring):
                outs[h][pl.ds(t * batch, batch)] = got[h * (ring - 1) + t - 1][...]

    shape = jax.ShapeDtypeStruct((ring * batch, *tail), column.dtype)
    return pl.pallas_call(kernel, out_shape=(shape, shape), name="assemble")(column, *parts)


def contract(plan, s, rows, sibling, amps, slot_pair, meta):
    width, lanes = rows.shape[1], rows.shape[2]
    side = width // 2
    batch, ring = plan.batch, plan.ring

    def kernel(sp, where, *refs):
        own, (sib, amp_0, amp_1, out_0, out_1, token, wide, held) = refs[:batch], refs[batch:]
        g = pl.program_id(0)
        low = lax.broadcasted_iota(jnp.int32, (side, lanes), 1) < lanes // 2
        zero = jnp.zeros((width, lanes), BF16)
        none = jnp.zeros((side, lanes), F32)

        @pl.when(g < ring)
        def _():
            held[...] = amp_0[...]

        @pl.when(g >= ring)
        def _():
            held[...] = amp_1[...]

        for n in range(batch):
            base = n * 2 * width
            wide[pl.ds(base, width), :] = own[n][0].astype(F32)
            wide[pl.ds(base + width, width), :] = sib[n].astype(F32)
            parts = [
                wide[pl.ds(base + u * width + p, side, stride=2), :] for u in range(2) for p in range(2)
            ]
            left = jnp.concatenate(parts, axis=0).astype(BF16)
            amp_n = held[n]
            right = jnp.concatenate(
                [
                    jnp.concatenate([amp_n, zero], axis=1),
                    jnp.concatenate([zero, amp_n], axis=1),
                ],
                axis=0,
            )
            inner_w = jnp.dot(left, right, preferred_element_type=F32).astype(BF16)
            lhs = jnp.concatenate(
                [
                    jnp.concatenate(
                        [
                            inner_w[p * side : (p + 1) * side, u * lanes : (u + 1) * lanes]
                            for p in range(4)
                        ],
                        axis=1,
                    )
                    for u in range(2)
                ],
                axis=0,
            )
            cols = []
            for part in parts:
                turned = pltpu.roll(part, lanes // 2, 1)
                cols.append(
                    jnp.concatenate(
                        [
                            jnp.where(low, part, none),
                            jnp.where(low, turned, none),
                            jnp.where(low, none, turned),
                            jnp.where(low, none, part),
                        ],
                        axis=0,
                    ).astype(BF16)
                )
            rhs = jnp.concatenate(cols, axis=1)
            held[n] = lax.dot_general(
                lhs, rhs, (((1,), (1,)), ((), ())), preferred_element_type=F32
            ).astype(BF16)

        @pl.when(g < ring)
        def _():
            out_0[...] = held[...]

        @pl.when(g >= ring)
        def _():
            out_1[...] = held[...]

        for i in range(4):
            token[i] = where[i]

    def own_spec(n):
        def where_is(g, sp, where):
            return sp[plan.slot(s, g, n, where, where[3])], 0, 0

        return pl.BlockSpec((1, width, lanes), where_is)

    block = (batch, width, lanes)
    first = pl.BlockSpec(block, lambda g, sp, where: (jnp.minimum(g, ring - 1), 0, 0))
    second = pl.BlockSpec(block, lambda g, sp, where: (jnp.maximum(g - ring, 0), 0, 0))
    count = ring * batch
    shape = jax.ShapeDtypeStruct((count, width, lanes), BF16)
    return pl.pallas_call(
        kernel,
        grid_spec=pltpu.PrefetchScalarGridSpec(
            num_scalar_prefetch=2,
            grid=(plan.rows,),
            in_specs=[own_spec(n) for n in range(batch)]
            + [
                pl.BlockSpec(block, lambda g, sp, where: (s * plan.rows + g, 0, 0)),
                first,
                second,
            ],
            out_specs=(first, second, pl.BlockSpec(memory_space=pltpu.SMEM)),
            scratch_shapes=[pltpu.VMEM((batch * 2 * width, lanes), F32), pltpu.VMEM(block, BF16)],
        ),
        out_shape=(shape, shape, jax.ShapeDtypeStruct((4,), jnp.int32)),
        cost_estimate=pl.CostEstimate(
            flops=2 * count * 4 * (128 * 128 * 256),
            bytes_accessed=2 * count * 65536,
            transcendentals=0,
        ),
        name="contract",
    )(slot_pair, meta, *([rows] * batch), sibling, *amps)


def finish(line, amps, denom, square):
    nz, local, width, lanes = line.shape
    side = width // 2

    def kernel(line_ref, amp_ref, den_ref, sq_ref, res_ref, new_ref, wide, part):
        source = lax.broadcasted_iota(jnp.int32, (lanes, lanes), 0)
        target = lax.broadcasted_iota(jnp.int32, (lanes, lanes), 1)
        col = target % width
        for i in range(local):
            total = line_ref[0, i].astype(F32)
            for z in range(1, nz):
                total = total + line_ref[z, i].astype(F32)
            wide[...] = amp_ref[i].astype(F32)
            den, sq = den_ref[i], sq_ref[i]
            for k in range(2):
                value = jnp.zeros((side, lanes), F32)
                for u in range(2):
                    chosen = (target // width == u) & (
                        source == k * width + (col % 2) * side + col // 2
                    )
                    value = value + jnp.dot(
                        total[u * side : (u + 1) * side],
                        chosen.astype(F32),
                        precision=lax.Precision.HIGHEST,
                        preferred_element_type=F32,
                    )
                value = value * sq
                amp = wide[pl.ds(k, side, stride=2), :] * sq
                part[pl.ds(k, side, stride=2), :] = value
                wide[pl.ds(k, side, stride=2), :] = (amp - value / den) * sq
            res_ref[i] = part[...]
            new_ref[i] = wide[...].astype(BF16)

    shape = (local, width, lanes)
    return pl.pallas_call(
        kernel,
        out_shape=(jax.ShapeDtypeStruct(shape, F32), jax.ShapeDtypeStruct(shape, BF16)),
        scratch_shapes=[pltpu.VMEM((width, lanes), F32), pltpu.VMEM((width, lanes), F32)],
        name="finish",
    )(line, amps, denom, square)


def total_of(values):
    summed = values[0].astype(F32)
    for value in values[1:]:
        summed = summed + value.astype(F32)
    return summed


def body(ints_ac, slot_pair, amplitudes, ranks, pair_occ, pno_energy, occ_energy):
    width = pno_energy.shape[1]
    local = amplitudes.shape[0]
    lanes = 2 * width
    plan = Plan(tuple(lax.axis_size(a) for a in AXES), local)
    meta = jnp.stack([lax.axis_index(a) for a in AXES]).astype(jnp.int32)

    positions = jnp.arange(width, dtype=jnp.int32)
    masks = (positions[None, :] < ranks[:, None]).astype(F32)
    square = masks[:, :, None] * masks[:, None, :]
    masked_t = amplitudes.astype(F32).reshape(local, 2, width, width) * square[:, None]

    def paired(value):
        value = value.reshape(value.shape[0], 2, width // 2, lanes).transpose(0, 2, 1, 3)
        return value.reshape(value.shape[0], width, lanes)

    def unpaired(value):
        value = value.reshape(local, width // 2, 2, lanes).transpose(0, 2, 1, 3)
        return value.reshape(local, 2, width * width)

    rows = paired(ints_ac)

    mine = masked_t.astype(BF16).transpose(0, 2, 1, 3).reshape(local, width, lanes)
    nz, ring = plan.nz, plan.ring
    column = lax.all_to_all(
        jnp.broadcast_to(mine, (nz, *mine.shape)), "z", split_axis=0, concat_axis=0, tiled=True
    )
    column = column.reshape(nz * local, width, lanes)

    sent = collect(plan, rows, slot_pair, meta)
    sibling = moved(sent, "core", 1)

    short, long = ("x", "y"), ("y", "x")
    pieces = [column[h * plan.batch : (h + 1) * plan.batch] for h in range(2)]
    parts = [moved(pieces[h], short[h], t) for h in range(2) for t in range(1, ring)]
    planes = assemble(plan, column, parts)
    arrived = [planes] + [
        tuple(moved(planes[h], long[h], s) for h in range(2)) for s in range(1, ring)
    ]
    back = [[], []]
    token = meta
    for s in range(ring):
        *partial, token = contract(plan, s, rows, sibling, arrived[s], slot_pair, token)
        for h in range(2):
            back[h].append(moved(partial[h], long[h], -s) if s else partial[h])
    halves = []
    for h in range(2):
        plane = total_of(back[h]).astype(BF16).reshape(ring, plan.batch, width, lanes)
        last = [plane[0]] + [moved(plane[t], short[h], -t) for t in range(1, ring)]
        halves.append(total_of(last).astype(BF16))
    line = jnp.concatenate(halves, axis=0).reshape(nz, local, width, lanes)
    line = lax.all_to_all(line, "z", split_axis=0, concat_axis=0, tiled=True)

    onehot = (
        pair_occ[:, :, None] == jnp.arange(occ_energy.shape[0], dtype=jnp.int32)[None, None, :]
    ).astype(F32)
    occ_pair = jnp.einsum("jko,o->jk", onehot, occ_energy, precision=lax.Precision.HIGHEST)
    denom = (
        pno_energy[:, :, None]
        + pno_energy[:, None, :]
        - (occ_pair[:, 0] + occ_pair[:, 1])[:, None, None]
    )
    flat = (local, width // 2, lanes)
    residual, updated = finish(line, paired(amplitudes), denom.reshape(flat), square.reshape(flat))
    return unpaired(residual), unpaired(updated)


def solution(mesh):
    fine = Mesh(mesh.devices.reshape(-1, *SIDES), AXES)
    placed = (
        P(None, AXES, None),
        P(),
        P(AXES, None, None),
        P(AXES),
        P(AXES, None),
        P(AXES, None),
        P(),
    )
    return jax.shard_map(
        body,
        mesh=fine,
        in_specs=placed,
        out_specs=(P(AXES, None, None), P(AXES, None, None)),
        check_vma=False,
    )
```

profile of v0, /device:TPU:24, one launch (start us, length us, event | category | flops | bytes accessed | tf_op | source)
XLA Modules:
  0.0 244.7 jit_solution(5203857415044195840)
XLA Ops:
  0.7 0.6 pad_add_fusion.where
  1.3 20.1 %collect.1 = bf16[384,64,128]{2,1,0:T(8,128)(2,1)} custom-call(s32[768]{0:T(1024)} %sp.9, s32[4]{0:T(128)} %pad_add_fusion.where, bf16[768,64,128]{2,1,0:T(8,128)(2,1)} %bitcast.47, bf16[768,64,128]{2,1,0:T(8,128)(2,1)} %bitcast.37, bf16[768,64,128]{2,1,0:T(8,128)(2,1)} %bitcast.38, bf16[768,64,128]{2,1,0:T(8,128)(2,1)} %bitcast.39, ...), custom_call_target="tpu_custom_call" | custom-call | flops 384000000 | bytes 12582912 | tf_op jit(solution)/shard_map/collect/pallas_call | solution.py:55
  21.8 0.6 copy-done.3
  22.8 23.6 %all_to_all.10 = bf16[8,3,64,128]{3,2,1,0:T(8,128)(2,1)S(1)} all-to-all(bf16[8,3,64,128]{3,2,1,0:T(8,128)(2,1)S(1)} %broadcast_in_dim.2), channel_id=1, replica_groups=mesh['z'=8,'y'=4,'x'=4,'core'=2] {'z'}, dimensions={0} | all-to-all | bytes 786432 | tf_op jit(solution)/shard_map/all_to_all | solution.py:274
  46.4 1.6 collective-permute-start.1
  48.0 2.7 %collective-permute-start.2 = (bf16[12,64,128]{2,1,0:T(8,128)(2,1)S(1)}, bf16[12,64,128]{2,1,0:T(8,128)(2,1)S(1)}, u32[]{:S(2)}, u32[]{:S(2)}) collective-permute-start(bf16[12,64,128]{2,1,0:T(8,128)(2,1)S(1)} %bitcast.101), channel_id=1, source_target_pairs={{0,4},{2,6},{4,0},{6,2},{1,5},{3,7},{5,1},{7,3},{8,12},{10,14},{12... | collective-permute-start | bytes 589832 | tf_op jit(solution)/shard_map/ppermute | solution.py:16
  50.7 1.4 collective-permute-start.3
  52.4 2.2 collective-permute-done.1.refs_0_
  54.6 1.2 collective-permute-start.5
  55.8 4.0 %collective-permute-done.2.refs_1_ = bf16[12,64,128]{2,1,0:T(8,128)(2,1)S(1)} collective-permute-done((bf16[12,64,128]{2,1,0:T(8,128)(2,1)S(1)}, bf16[12,64,128]{2,1,0:T(8,128)(2,1)S(1)}, u32[]{:S(2)}, u32[]{:S(2)}) %collective-permute-start.2) | collective-permute-done | bytes 196640 | tf_op jit(solution)/shard_map/ppermute | solution.py:16
  59.8 0.7 collective-permute-start.6
  60.5 2.4 collective-permute-done.5.refs_4_
  62.9 4.1 %collective-permute-done.6.refs_5_ = bf16[12,64,128]{2,1,0:T(8,128)(2,1)S(1)} collective-permute-done((bf16[12,64,128]{2,1,0:T(8,128)(2,1)S(1)}, bf16[12,64,128]{2,1,0:T(8,128)(2,1)S(1)}, u32[]{:S(2)}, u32[]{:S(2)}) %collective-permute-start.6) | collective-permute-done | bytes 196640 | tf_op jit(solution)/shard_map/ppermute | solution.py:16
  67.1 0.6 copy-done.17
  67.7 2.6 %assemble.1 = (bf16[48,64,128]{2,1,0:T(8,128)(2,1)}, bf16[48,64,128]{2,1,0:T(8,128)(2,1)}) custom-call(bf16[24,64,128]{2,1,0:T(8,128)(2,1)} %bitcast.96, bf16[12,64,128]{2,1,0:T(8,128)(2,1)} %copy-done.12, bf16[12,64,128]{2,1,0:T(8,128)(2,1)} %copy-done.13, bf16[12,64,128]{2,1,0:T(8,128)(2,1)} %copy-done.14, bf16[12,64,128]{2,1,0:T(8,128)(2,1)} %copy-done.15, ...), custom_call_target="tpu_custom_call" | custom-call | tf_op jit(solution)/shard_map/assemble/pallas_call | solution.py:83
  70.5 1.4 collective-permute-start.10
  71.9 2.5 %collective-permute-start.11 = (bf16[48,64,128]{2,1,0:T(8,128)(2,1)}, bf16[48,64,128]{2,1,0:T(8,128)(2,1)S(1)}, u32[]{:S(2)}, u32[]{:S(2)}) collective-permute-start(bf16[48,64,128]{2,1,0:T(8,128)(2,1)} %get-tuple-element.18.refs_14_), channel_id=1, source_target_pairs={{0,4},{2,6},{4,0},{6,2},{1,5},{3,7},{5,1},{7,3},{8,12},{10,14},{12... | collective-permute-start | bytes 2359304 | tf_op jit(solution)/shard_map/ppermute | solution.py:16
  74.4 16.6 %collective-permute-done.7.refs_13_ = bf16[48,64,128]{2,1,0:T(8,128)(2,1)S(1)} collective-permute-done((bf16[48,64,128]{2,1,0:T(8,128)(2,1)}, bf16[48,64,128]{2,1,0:T(8,128)(2,1)S(1)}, u32[]{:S(2)}, u32[]{:S(2)}) %collective-permute-start.7) | collective-permute-done | bytes 786464 | tf_op jit(solution)/shard_map/ppermute | solution.py:16
  91.0 0.9 copy-done.9
  91.9 0.8 collective-permute-start.14
  92.7 16.5 %contract.4 = (bf16[48,64,128]{2,1,0:T(8,128)(2,1)}, bf16[48,64,128]{2,1,0:T(8,128)(2,1)}, s32[4]{0:T(128)}) custom-call(s32[768]{0:T(1024)} %sp.9, s32[4]{0:T(128)} %pad_add_fusion.where, bf16[768,64,128]{2,1,0:T(8,128)(2,1)} %bitcast.48, bf16[768,64,128]{2,1,0:T(8,128)(2,1)} %bitcast.49, bf16[768,64,128]{2,1,0:T(8,128)(2,1)} %bitcast.50, ...), custom_call_target="tpu_custom_call" | custom-call | flops 1610612736 | bytes 6291456 | tf_op jit(solution)/shard_map/contract/pallas_call | solution.py:177
  109.2 16.5 %contract.5 = (bf16[48,64,128]{2,1,0:T(8,128)(2,1)}, bf16[48,64,128]{2,1,0:T(8,128)(2,1)}, s32[4]{0:T(128)}) custom-call(s32[768]{0:T(1024)} %sp.9, s32[4]{0:T(128)} %get-tuple-element.20.where, bf16[768,64,128]{2,1,0:T(8,128)(2,1)} %bitcast.65, bf16[768,64,128]{2,1,0:T(8,128)(2,1)} %bitcast.61, bf16[768,64,128]{2,1,0:T(8,128)(2,1)} %bitcast.62, ...), custom_call_target="tpu_custom_call" | custom-call | flops 1610612736 | bytes 6291456 | tf_op jit(solution)/shard_map/contract/pallas_call | solution.py:177
  125.8 0.9 copy-done.6
  127.0 16.5 %contract.6 = (bf16[48,64,128]{2,1,0:T(8,128)(2,1)}, bf16[48,64,128]{2,1,0:T(8,128)(2,1)}, s32[4]{0:T(128)}) custom-call(s32[768]{0:T(1024)} %sp.9, s32[4]{0:T(128)} %get-tuple-element.22.where, bf16[768,64,128]{2,1,0:T(8,128)(2,1)} %bitcast.78, bf16[768,64,128]{2,1,0:T(8,128)(2,1)} %bitcast.73, bf16[768,64,128]{2,1,0:T(8,128)(2,1)} %bitcast.74, ...), custom_call_target="tpu_custom_call" | custom-call | flops 1610612736 | bytes 6291456 | tf_op jit(solution)/shard_map/contract/pallas_call | solution.py:177
  143.6 0.9 copy-done.5
  144.7 16.7 %contract.7 = (bf16[48,64,128]{2,1,0:T(8,128)(2,1)}, bf16[48,64,128]{2,1,0:T(8,128)(2,1)}, s32[4]{0:T(128)}) custom-call(s32[768]{0:T(1024)} %sp.9, s32[4]{0:T(128)} %get-tuple-element.24.where, bf16[768,64,128]{2,1,0:T(8,128)(2,1)} %bitcast.84, bf16[768,64,128]{2,1,0:T(8,128)(2,1)} %bitcast.85, bf16[768,64,128]{2,1,0:T(8,128)(2,1)} %bitcast.86, ...), custom_call_target="tpu_custom_call" | custom-call | flops 1610612736 | bytes 6291456 | tf_op jit(solution)/shard_map/contract/pallas_call | solution.py:177
  161.4 1.3 collective-permute-start.21
  162.7 2.2 collective-permute-start.20
  164.9 0.6 collective-permute-start.19
  165.6 2.4 collective-permute-start.15
  167.9 13.2 %collective-permute-done.21 = bf16[48,64,128]{2,1,0:T(8,128)(2,1)S(1)} collective-permute-done((bf16[48,64,128]{2,1,0:T(8,128)(2,1)}, bf16[48,64,128]{2,1,0:T(8,128)(2,1)S(1)}, u32[]{:S(2)}, u32[]{:S(2)}) %collective-permute-start.21) | collective-permute-done | bytes 786464 | tf_op jit(solution)/shard_map/ppermute | solution.py:16
  181.2 0.7 collective-permute-start.9
  181.8 14.0 %collective-permute-done.20 = bf16[48,64,128]{2,1,0:T(8,128)(2,1)S(1)} collective-permute-done((bf16[48,64,128]{2,1,0:T(8,128)(2,1)}, bf16[48,64,128]{2,1,0:T(8,128)(2,1)S(1)}, u32[]{:S(2)}, u32[]{:S(2)}) %collective-permute-start.20) | collective-permute-done | bytes 786464 | tf_op jit(solution)/shard_map/ppermute | solution.py:16
  196.5 2.1 collective-permute-start.24
  199.0 1.0 collective-permute-start.22
  200.0 1.6 collective-permute-done.9
  201.5 0.6 add_convert_fusion.1
  202.2 10.0 %collective-permute-start.18 = (bf16[12,64,128]{2,1,0:T(8,128)(2,1)S(1)}, bf16[12,64,128]{2,1,0:T(8,128)(2,1)S(1)}, u32[]{:S(2)}, u32[]{:S(2)}) collective-permute-start(bf16[12,64,128]{2,1,0:T(8,128)(2,1)S(1)} %get-tuple-element.33), channel_id=1, source_target_pairs={{0,2},{2,4},{4,6},{6,0},{1,3},{3,5},{5,7},{7,1},{8,10},{10,12},{12... | collective-permute-start | bytes 589832 | tf_op jit(solution)/shard_map/ppermute | solution.py:16
  212.2 2.4 collective-permute-start.17
  214.6 2.5 %collective-permute-start.16 = (bf16[12,64,128]{2,1,0:T(8,128)(2,1)S(1)}, bf16[12,64,128]{2,1,0:T(8,128)(2,1)S(1)}, u32[]{:S(2)}, u32[]{:S(2)}) collective-permute-start(bf16[12,64,128]{2,1,0:T(8,128)(2,1)S(1)} %get-tuple-element.32), channel_id=1, source_target_pairs={{0,6},{2,0},{4,2},{6,4},{1,7},{3,1},{5,3},{7,5},{8,14},{10,8},{12,... | collective-permute-start | bytes 589832 | tf_op jit(solution)/shard_map/ppermute | solution.py:16
  217.3 3.0 %collective-permute-done.17 = bf16[12,64,128]{2,1,0:T(8,128)(2,1)S(1)} collective-permute-done((bf16[12,64,128]{2,1,0:T(8,128)(2,1)S(1)}, bf16[12,64,128]{2,1,0:T(8,128)(2,1)S(1)}, u32[]{:S(2)}, u32[]{:S(2)}) %collective-permute-start.17) | collective-permute-done | bytes 196640 | tf_op jit(solution)/shard_map/ppermute | solution.py:16
  220.4 0.8 pad_maximum_fusion
  221.2 8.4 %all-to-all-start.1 = ((bf16[8,3,64,128]{3,2,1,0:T(8,128)(2,1)}), bf16[8,3,64,128]{3,2,1,0:T(8,128)(2,1)S(1)}, u32[]{:S(2)}, u32[]{:S(2)}) async-start(bf16[8,3,64,128]{3,2,1,0:T(8,128)(2,1)} %bitcast.13), calls=%async_computation.1 | async-start | bytes 786432 | tf_op jit(solution)/shard_map/all_to_all | solution.py:301
  229.7 0.7 mul.34.sq_ref
  230.9 0.7 broadcast_subtract_fusion.den_ref
  231.7 9.8 %all-to-all-done.1.line_ref = bf16[8,3,64,128]{3,2,1,0:T(8,128)(2,1)S(1)} async-done(((bf16[8,3,64,128]{3,2,1,0:T(8,128)(2,1)}), bf16[8,3,64,128]{3,2,1,0:T(8,128)(2,1)S(1)}, u32[]{:S(2)}, u32[]{:S(2)}) %all-to-all-start.1) | async-done | bytes 393248 | tf_op jit(solution)/shard_map/all_to_all | solution.py:301
  241.5 0.8 copy-done.2
  242.3 2.5 %finish.1 = (f32[3,64,128]{2,1,0:T(8,128)}, bf16[3,64,128]{2,1,0:T(8,128)(2,1)}) custom-call(bf16[8,3,64,128]{3,2,1,0:T(8,128)(2,1)} %copy-done.2, bf16[3,64,128]{2,1,0:T(8,128)(2,1)} %bitcast.103, f32[3,32,128]{2,1,0:T(8,128)} %broadcast_subtract_fusion.den_ref, f32[3,32,128]{2,1,0:T(8,128)} %mul.34.sq_ref), custom_call_target="tpu_custom_call" | custom-call | tf_op jit(solution)/shard_map/finish/pallas_call | solution.py:235
  (82 shorter events, 3.5 us)
Async XLA Ops:
  0.6 230.0 %copy-start = (f32[48]{0:T(128)S(1)}, f32[48]{0:T(128)}, u32[]{:S(2)}) copy-start(f32[48]{0:T(128)} %param.13) | copy-start | bytes 580
  1.3 20.2 %copy-start.18 = (bf16[3,2,4096]{2,1,0:T(2,128)(2,1)S(1)}, bf16[3,2,4096]{2,1,0:T(2,128)(2,1)}, u32[]{:S(2)}) copy-start(bf16[3,2,4096]{2,1,0:T(2,128)(2,1)} %param.9) | copy-start | bytes 147460
  1.3 20.4 %copy-start.21 = (s32[3]{0:T(128)S(1)}, s32[3]{0:T(128)}, u32[]{:S(2)}) copy-start(s32[3]{0:T(128)} %param.10) | copy-start | bytes 40
  21.4 70.5 %collective-permute-start = (bf16[384,64,128]{2,1,0:T(8,128)(2,1)}, bf16[384,64,128]{2,1,0:T(8,128)(2,1)}, u32[]{:S(2)}, u32[]{:S(2)}) collective-permute-start(bf16[384,64,128]{2,1,0:T(8,128)(2,1)} %collect.1), channel_id=1, source_target_pairs={{0,1},{1,0},{2,3},{3,2},{4,5},{5,4},{6,7},{7,6},{8,9},{9,8},{10,11... | collective-permute-start | bytes 18874376 | tf_op jit(solution)/shard_map/ppermute | solution.py:16
  46.4 20.7 %copy-start.1 = (bf16[8,3,64,128]{3,2,1,0:T(8,128)(2,1)}, bf16[8,3,64,128]{3,2,1,0:T(8,128)(2,1)S(1)}, u32[]{:S(2)}) copy-start(bf16[8,3,64,128]{3,2,1,0:T(8,128)(2,1)S(1)} %all_to_all.10) | copy-start | bytes 1179652
  46.4 8.1 %collective-permute-start.1 = (bf16[12,64,128]{2,1,0:T(8,128)(2,1)S(1)}, bf16[12,64,128]{2,1,0:T(8,128)(2,1)S(1)}, u32[]{:S(2)}, u32[]{:S(2)}) collective-permute-start(bf16[12,64,128]{2,1,0:T(8,128)(2,1)S(1)} %bitcast.100), channel_id=1, source_target_pairs={{0,2},{2,4},{4,6},{6,0},{1,3},{3,5},{5,7},{7,1},{8,10},{10,12},{12... | collective-permute-start | bytes 589832 | tf_op jit(solution)/shard_map/ppermute | solution.py:16
  48.0 11.8 %collective-permute-start.2 = (bf16[12,64,128]{2,1,0:T(8,128)(2,1)S(1)}, bf16[12,64,128]{2,1,0:T(8,128)(2,1)S(1)}, u32[]{:S(2)}, u32[]{:S(2)}) collective-permute-start(bf16[12,64,128]{2,1,0:T(8,128)(2,1)S(1)} %bitcast.101), channel_id=1, source_target_pairs={{0,4},{2,6},{4,0},{6,2},{1,5},{3,7},{5,1},{7,3},{8,12},{10,14},{12... | collective-permute-start | bytes 589832 | tf_op jit(solution)/shard_map/ppermute | solution.py:16
  50.7 9.8 %collective-permute-start.3 = (bf16[12,64,128]{2,1,0:T(8,128)(2,1)S(1)}, bf16[12,64,128]{2,1,0:T(8,128)(2,1)S(1)}, u32[]{:S(2)}, u32[]{:S(2)}) collective-permute-start(bf16[12,64,128]{2,1,0:T(8,128)(2,1)S(1)} %bitcast.102), channel_id=1, source_target_pairs={{0,6},{2,0},{4,2},{6,4},{1,7},{3,1},{5,3},{7,5},{8,14},{10,8},{12,... | collective-permute-start | bytes 589832 | tf_op jit(solution)/shard_map/ppermute | solution.py:16
  52.2 8.4 %collective-permute-start.4 = (bf16[12,64,128]{2,1,0:T(8,128)(2,1)S(1)}, bf16[12,64,128]{2,1,0:T(8,128)(2,1)S(1)}, u32[]{:S(2)}, u32[]{:S(2)}) collective-permute-start(bf16[12,64,128]{2,1,0:T(8,128)(2,1)S(1)} %bitcast.97), channel_id=1, source_target_pairs={{0,8},{8,16},{16,24},{24,0},{1,9},{9,17},{17,25},{25,1},{2,10},{10... | collective-permute-start | bytes 589832 | tf_op jit(solution)/shard_map/ppermute | solution.py:16
  54.6 12.5 %copy-start.12 = (bf16[12,64,128]{2,1,0:T(8,128)(2,1)}, bf16[12,64,128]{2,1,0:T(8,128)(2,1)S(1)}, u32[]{:S(2)}) copy-start(bf16[12,64,128]{2,1,0:T(8,128)(2,1)S(1)} %collective-permute-done.1.refs_0_) | copy-start | bytes 589828
  54.6 8.4 %collective-permute-start.5 = (bf16[12,64,128]{2,1,0:T(8,128)(2,1)S(1)}, bf16[12,64,128]{2,1,0:T(8,128)(2,1)S(1)}, u32[]{:S(2)}, u32[]{:S(2)}) collective-permute-start(bf16[12,64,128]{2,1,0:T(8,128)(2,1)S(1)} %bitcast.98), channel_id=1, source_target_pairs={{0,16},{8,24},{16,0},{24,8},{1,17},{9,25},{17,1},{25,9},{2,18},{10... | collective-permute-start | bytes 589832 | tf_op jit(solution)/shard_map/ppermute | solution.py:16
  59.8 7.3 %copy-start.13 = (bf16[12,64,128]{2,1,0:T(8,128)(2,1)}, bf16[12,64,128]{2,1,0:T(8,128)(2,1)S(1)}, u32[]{:S(2)}) copy-start(bf16[12,64,128]{2,1,0:T(8,128)(2,1)S(1)} %collective-permute-done.2.refs_1_) | copy-start | bytes 589828
  59.8 7.3 %collective-permute-start.6 = (bf16[12,64,128]{2,1,0:T(8,128)(2,1)S(1)}, bf16[12,64,128]{2,1,0:T(8,128)(2,1)S(1)}, u32[]{:S(2)}, u32[]{:S(2)}) collective-permute-start(bf16[12,64,128]{2,1,0:T(8,128)(2,1)S(1)} %bitcast.99), channel_id=1, source_target_pairs={{0,24},{8,0},{16,8},{24,16},{1,25},{9,1},{17,9},{25,17},{2,26},{10... | collective-permute-start | bytes 589832 | tf_op jit(solution)/shard_map/ppermute | solution.py:16
  60.5 6.6 %copy-start.14 = (bf16[12,64,128]{2,1,0:T(8,128)(2,1)}, bf16[12,64,128]{2,1,0:T(8,128)(2,1)S(1)}, u32[]{:S(2)}) copy-start(bf16[12,64,128]{2,1,0:T(8,128)(2,1)S(1)} %collective-permute-done.3.refs_2_) | copy-start | bytes 589828
  60.5 6.6 %copy-start.15 = (bf16[12,64,128]{2,1,0:T(8,128)(2,1)}, bf16[12,64,128]{2,1,0:T(8,128)(2,1)S(1)}, u32[]{:S(2)}) copy-start(bf16[12,64,128]{2,1,0:T(8,128)(2,1)S(1)} %collective-permute-done.4.refs_3_) | copy-start | bytes 589828
  62.9 4.2 %copy-start.16 = (bf16[12,64,128]{2,1,0:T(8,128)(2,1)}, bf16[12,64,128]{2,1,0:T(8,128)(2,1)S(1)}, u32[]{:S(2)}) copy-start(bf16[12,64,128]{2,1,0:T(8,128)(2,1)S(1)} %collective-permute-done.5.refs_4_) | copy-start | bytes 589828
  67.1 0.7 copy-start.17
  70.4 20.6 %collective-permute-start.7 = (bf16[48,64,128]{2,1,0:T(8,128)(2,1)}, bf16[48,64,128]{2,1,0:T(8,128)(2,1)S(1)}, u32[]{:S(2)}, u32[]{:S(2)}) collective-permute-start(bf16[48,64,128]{2,1,0:T(8,128)(2,1)} %get-tuple-element.17.refs_13_), channel_id=1, source_target_pairs={{0,8},{8,16},{16,24},{24,0},{1,9},{9,17},{17,25},{25,1},{2,10},{10... | collective-permute-start | bytes 2359304 | tf_op jit(solution)/shard_map/ppermute | solution.py:16
  70.4 38.8 %collective-permute-start.8 = (bf16[48,64,128]{2,1,0:T(8,128)(2,1)}, bf16[48,64,128]{2,1,0:T(8,128)(2,1)}, u32[]{:S(2)}, u32[]{:S(2)}) collective-permute-start(bf16[48,64,128]{2,1,0:T(8,128)(2,1)} %get-tuple-element.18.refs_14_), channel_id=1, source_target_pairs={{0,2},{2,4},{4,6},{6,0},{1,3},{3,5},{5,7},{7,1},{8,10},{10,12},{12... | collective-permute-start | bytes 2359304 | tf_op jit(solution)/shard_map/ppermute | solution.py:16
  70.5 55.3 %collective-permute-start.10 = (bf16[48,64,128]{2,1,0:T(8,128)(2,1)}, bf16[48,64,128]{2,1,0:T(8,128)(2,1)S(1)}, u32[]{:S(2)}, u32[]{:S(2)}) collective-permute-start(bf16[48,64,128]{2,1,0:T(8,128)(2,1)} %get-tuple-element.17.refs_13_), channel_id=1, source_target_pairs={{0,16},{8,24},{16,0},{24,8},{1,17},{9,25},{17,1},{25,9},{2,18},{10... | collective-permute-start | bytes 2359304 | tf_op jit(solution)/shard_map/ppermute | solution.py:16
  71.9 53.9 %collective-permute-start.11 = (bf16[48,64,128]{2,1,0:T(8,128)(2,1)}, bf16[48,64,128]{2,1,0:T(8,128)(2,1)S(1)}, u32[]{:S(2)}, u32[]{:S(2)}) collective-permute-start(bf16[48,64,128]{2,1,0:T(8,128)(2,1)} %get-tuple-element.18.refs_14_), channel_id=1, source_target_pairs={{0,4},{2,6},{4,0},{6,2},{1,5},{3,7},{5,1},{7,3},{8,12},{10,14},{12... | collective-permute-start | bytes 2359304 | tf_op jit(solution)/shard_map/ppermute | solution.py:16
  91.0 0.9 copy-start.9
  91.0 52.5 %collective-permute-start.13 = (bf16[48,64,128]{2,1,0:T(8,128)(2,1)}, bf16[48,64,128]{2,1,0:T(8,128)(2,1)S(1)}, u32[]{:S(2)}, u32[]{:S(2)}) collective-permute-start(bf16[48,64,128]{2,1,0:T(8,128)(2,1)} %get-tuple-element.17.refs_13_), channel_id=1, source_target_pairs={{0,24},{8,0},{16,8},{24,16},{1,25},{9,1},{17,9},{25,17},{2,26},{10... | collective-permute-start | bytes 2359304 | tf_op jit(solution)/shard_map/ppermute | solution.py:16
  91.9 51.6 %collective-permute-start.14 = (bf16[48,64,128]{2,1,0:T(8,128)(2,1)}, bf16[48,64,128]{2,1,0:T(8,128)(2,1)S(1)}, u32[]{:S(2)}, u32[]{:S(2)}) collective-permute-start(bf16[48,64,128]{2,1,0:T(8,128)(2,1)} %get-tuple-element.18.refs_14_), channel_id=1, source_target_pairs={{0,6},{2,0},{4,2},{6,4},{1,7},{3,1},{5,3},{7,5},{8,14},{10,8},{12,... | collective-permute-start | bytes 2359304 | tf_op jit(solution)/shard_map/ppermute | solution.py:16
  125.8 0.9 copy-start.6
  125.8 1.2 copy-start.8
  143.5 0.9 copy-start.5
  143.6 1.1 copy-start.7
  144.7 36.5 %copy-start.22 = (bf16[48,64,128]{2,1,0:T(8,128)(2,1)S(1)}, bf16[48,64,128]{2,1,0:T(8,128)(2,1)}, u32[]{:S(2)}) copy-start(bf16[48,64,128]{2,1,0:T(8,128)(2,1)} %get-tuple-element.21) | copy-start | bytes 2359300
  144.7 51.1 %copy-start.11 = (bf16[48,64,128]{2,1,0:T(8,128)(2,1)S(1)}, bf16[48,64,128]{2,1,0:T(8,128)(2,1)}, u32[]{:S(2)}) copy-start(bf16[48,64,128]{2,1,0:T(8,128)(2,1)} %get-tuple-element.26) | copy-start | bytes 2359300
  161.4 19.8 %collective-permute-start.21 = (bf16[48,64,128]{2,1,0:T(8,128)(2,1)}, bf16[48,64,128]{2,1,0:T(8,128)(2,1)S(1)}, u32[]{:S(2)}, u32[]{:S(2)}) collective-permute-start(bf16[48,64,128]{2,1,0:T(8,128)(2,1)} %get-tuple-element.29), channel_id=1, source_target_pairs={{0,2},{2,4},{4,6},{6,0},{1,3},{3,5},{5,7},{7,1},{8,10},{10,12},{12... | collective-permute-start | bytes 2359304 | tf_op jit(solution)/shard_map/ppermute | solution.py:16
  162.7 33.1 %collective-permute-start.20 = (bf16[48,64,128]{2,1,0:T(8,128)(2,1)}, bf16[48,64,128]{2,1,0:T(8,128)(2,1)S(1)}, u32[]{:S(2)}, u32[]{:S(2)}) collective-permute-start(bf16[48,64,128]{2,1,0:T(8,128)(2,1)} %get-tuple-element.28), channel_id=1, source_target_pairs={{0,4},{2,6},{4,0},{6,2},{1,5},{3,7},{5,1},{7,3},{8,12},{10,14},{12... | collective-permute-start | bytes 2359304 | tf_op jit(solution)/shard_map/ppermute | solution.py:16
  164.9 30.9 %collective-permute-start.19 = (bf16[48,64,128]{2,1,0:T(8,128)(2,1)}, bf16[48,64,128]{2,1,0:T(8,128)(2,1)S(1)}, u32[]{:S(2)}, u32[]{:S(2)}) collective-permute-start(bf16[48,64,128]{2,1,0:T(8,128)(2,1)} %get-tuple-element.27), channel_id=1, source_target_pairs={{0,6},{2,0},{4,2},{6,4},{1,7},{3,1},{5,3},{7,5},{8,14},{10,8},{12,... | collective-permute-start | bytes 2359304 | tf_op jit(solution)/shard_map/ppermute | solution.py:16
  165.6 33.4 %collective-permute-start.15 = (bf16[48,64,128]{2,1,0:T(8,128)(2,1)}, bf16[48,64,128]{2,1,0:T(8,128)(2,1)S(1)}, u32[]{:S(2)}, u32[]{:S(2)}) collective-permute-start(bf16[48,64,128]{2,1,0:T(8,128)(2,1)} %get-tuple-element.25), channel_id=1, source_target_pairs={{0,8},{8,16},{16,24},{24,0},{1,9},{9,17},{17,25},{25,1},{2,10},{10... | collective-permute-start | bytes 2359304 | tf_op jit(solution)/shard_map/ppermute | solution.py:16
  167.9 32.1 %collective-permute-start.12 = (bf16[48,64,128]{2,1,0:T(8,128)(2,1)}, bf16[48,64,128]{2,1,0:T(8,128)(2,1)S(1)}, u32[]{:S(2)}, u32[]{:S(2)}) collective-permute-start(bf16[48,64,128]{2,1,0:T(8,128)(2,1)} %get-tuple-element.23), channel_id=1, source_target_pairs={{0,16},{8,24},{16,0},{24,8},{1,17},{9,25},{17,1},{25,9},{2,18},{10... | collective-permute-start | bytes 2359304 | tf_op jit(solution)/shard_map/ppermute | solution.py:16
  181.2 20.4 %collective-permute-start.9 = (bf16[48,64,128]{2,1,0:T(8,128)(2,1)S(1)}, bf16[48,64,128]{2,1,0:T(8,128)(2,1)S(1)}, u32[]{:S(2)}, u32[]{:S(2)}) collective-permute-start(bf16[48,64,128]{2,1,0:T(8,128)(2,1)S(1)} %copy-done.22), channel_id=1, source_target_pairs={{0,24},{8,0},{16,8},{24,16},{1,25},{9,1},{17,9},{25,17},{2,26},{10... | collective-permute-start | bytes 2359304 | tf_op jit(solution)/shard_map/ppermute | solution.py:16
  196.5 5.1 %copy-start.10 = (bf16[48,64,128]{2,1,0:T(8,128)(2,1)S(1)}, bf16[48,64,128]{2,1,0:T(8,128)(2,1)}, u32[]{:S(2)}) copy-start(bf16[48,64,128]{2,1,0:T(8,128)(2,1)} %get-tuple-element.19) | copy-start | bytes 2359300
  196.5 18.1 %collective-permute-start.24 = (bf16[12,64,128]{2,1,0:T(8,128)(2,1)S(1)}, bf16[12,64,128]{2,1,0:T(8,128)(2,1)S(1)}, u32[]{:S(2)}, u32[]{:S(2)}) collective-permute-start(bf16[12,64,128]{2,1,0:T(8,128)(2,1)S(1)} %get-tuple-element.36), channel_id=1, source_target_pairs={{0,8},{8,16},{16,24},{24,0},{1,9},{9,17},{17,25},{25,1},{2,10},{10... | collective-permute-start | bytes 589832 | tf_op jit(solution)/shard_map/ppermute | solution.py:16
  198.7 18.5 %collective-permute-start.23 = (bf16[12,64,128]{2,1,0:T(8,128)(2,1)S(1)}, bf16[12,64,128]{2,1,0:T(8,128)(2,1)S(1)}, u32[]{:S(2)}, u32[]{:S(2)}) collective-permute-start(bf16[12,64,128]{2,1,0:T(8,128)(2,1)S(1)} %get-tuple-element.37), channel_id=1, source_target_pairs={{0,16},{8,24},{16,0},{24,8},{1,17},{9,25},{17,1},{25,9},{2,18},{10... | collective-permute-start | bytes 589832 | tf_op jit(solution)/shard_map/ppermute | solution.py:16
  199.0 18.2 %collective-permute-start.22 = (bf16[12,64,128]{2,1,0:T(8,128)(2,1)S(1)}, bf16[12,64,128]{2,1,0:T(8,128)(2,1)S(1)}, u32[]{:S(2)}, u32[]{:S(2)}) collective-permute-start(bf16[12,64,128]{2,1,0:T(8,128)(2,1)S(1)} %get-tuple-element.35), channel_id=1, source_target_pairs={{0,24},{8,0},{16,8},{24,16},{1,25},{9,1},{17,9},{25,17},{2,26},{10... | collective-permute-start | bytes 589832 | tf_op jit(solution)/shard_map/ppermute | solution.py:16
  202.2 15.1 %collective-permute-start.18 = (bf16[12,64,128]{2,1,0:T(8,128)(2,1)S(1)}, bf16[12,64,128]{2,1,0:T(8,128)(2,1)S(1)}, u32[]{:S(2)}, u32[]{:S(2)}) collective-permute-start(bf16[12,64,128]{2,1,0:T(8,128)(2,1)S(1)} %get-tuple-element.33), channel_id=1, source_target_pairs={{0,2},{2,4},{4,6},{6,0},{1,3},{3,5},{5,7},{7,1},{8,10},{10,12},{12... | collective-permute-start | bytes 589832 | tf_op jit(solution)/shard_map/ppermute | solution.py:16
  212.2 8.0 %collective-permute-start.17 = (bf16[12,64,128]{2,1,0:T(8,128)(2,1)S(1)}, bf16[12,64,128]{2,1,0:T(8,128)(2,1)S(1)}, u32[]{:S(2)}, u32[]{:S(2)}) collective-permute-start(bf16[12,64,128]{2,1,0:T(8,128)(2,1)S(1)} %get-tuple-element.34), channel_id=1, source_target_pairs={{0,4},{2,6},{4,0},{6,2},{1,5},{3,7},{5,1},{7,3},{8,12},{10,14},{12... | collective-permute-start | bytes 589832 | tf_op jit(solution)/shard_map/ppermute | solution.py:16
  214.6 15.0 %copy-start.19 = (f32[3,64]{1,0:T(4,128)S(1)}, f32[3,64]{1,0:T(4,128)}, u32[]{:S(2)}) copy-start(f32[3,64]{1,0:T(4,128)} %param.12) | copy-start | bytes 2308
  214.6 5.7 %collective-permute-start.16 = (bf16[12,64,128]{2,1,0:T(8,128)(2,1)S(1)}, bf16[12,64,128]{2,1,0:T(8,128)(2,1)S(1)}, u32[]{:S(2)}, u32[]{:S(2)}) collective-permute-start(bf16[12,64,128]{2,1,0:T(8,128)(2,1)S(1)} %get-tuple-element.32), channel_id=1, source_target_pairs={{0,6},{2,0},{4,2},{6,4},{1,7},{3,1},{5,3},{7,5},{8,14},{10,8},{12,... | collective-permute-start | bytes 589832 | tf_op jit(solution)/shard_map/ppermute | solution.py:16
  217.3 12.5 %copy-start.4 = (f32[3,64,64]{2,1,0:T(8,128)S(1)}, f32[3,64,64]{2,1,0:T(8,128)}, u32[]{:S(2)}) copy-start(f32[3,64,64]{2,1,0:T(8,128)} %copy-done.3) | copy-start | bytes 147460
  217.3 13.2 %copy-start.20 = (s32[3,2]{0,1:T(2,128)S(1)}, s32[3,2]{0,1:T(2,128)}, u32[]{:S(2)}) copy-start(s32[3,2]{0,1:T(2,128)} %param.11) | copy-start | bytes 76
  221.2 20.3 %all-to-all-start.1 = ((bf16[8,3,64,128]{3,2,1,0:T(8,128)(2,1)}), bf16[8,3,64,128]{3,2,1,0:T(8,128)(2,1)S(1)}, u32[]{:S(2)}, u32[]{:S(2)}) async-start(bf16[8,3,64,128]{3,2,1,0:T(8,128)(2,1)} %bitcast.13), calls=%async_computation.1 | async-start | bytes 786432 | tf_op jit(solution)/shard_map/all_to_all | solution.py:301
  241.5 0.8 copy-start.2
  (1 other events, 0.6 us)
where the time goes:
time: 248 us; the launch traced here: 245 us
  Pallas kernels  91.5 us (37%)
  waiting for transfers between devices  71 us (29%)
  starting transfers between devices  46.8 us (19%)
  blocking collectives  23.6 us (10%)
  local copies, waits for them, and re-layouts  6.8 us (3%)
  other arithmetic  3.9 us (2%)
    pallas_call x4, Pallas kernels, contract(): pl.pallas_call(kernel, grid_spec=pltpu.PrefetchScalarGridSpec(num_scalar_...  66.2 us
    ppermute x25, waiting for transfers between devices, moved(): return lax.ppermute(value, axis, [(j, (j + step) % n) for j in range(n)])  61.1 us
    ppermute x25, starting transfers between devices, moved(): return lax.ppermute(value, axis, [(j, (j + step) % n) for j in range(n)])  38.4 us
    all_to_all x1, blocking collectives, body(): lax.all_to_all(jnp.broadcast_to(mine, (nz, *mine.shape)), 'z', split_axis...  23.6 us
    pallas_call x1, Pallas kernels, collect(): pl.pallas_call(kernel, grid_spec=pltpu.PrefetchScalarGridSpec(num_scalar_...  20.1 us
    all_to_all x1, waiting for transfers between devices, body(): line = lax.all_to_all(line, 'z', split_axis=0, concat_axis=0, tiled=True)  9.85 us
    all_to_all x1, starting transfers between devices, body(): line = lax.all_to_all(line, 'z', split_axis=0, concat_axis=0, tiled=True)  8.39 us
    unnamed x47, local copies, waits for them, and re-layouts  5.41 us
  transfers between devices with their start and end apart: 26, of which 11 were waited for; matrix products, arithmetic and copies ran while one was open for 2% of the time, Pallas kernels for 21%

commit v1 on v0

--- a/solution.py
+++ b/solution.py
@@ -24,48 +24,56 @@
         self.local = local
         self.half = self.nz // 2
         self.batch = self.half * local
-        self.rows = 2 * self.ring
-
-    def slot(self, s, g, n, meta, core):
-        h, t = g // self.ring, g % self.ring
-        sy = jnp.where(h == 0, s, t)
-        sx = jnp.where(h == 0, t, s)
-        y = lax.rem(meta[1] - sy + self.ring, self.ring)
-        x = lax.rem(meta[2] - sx + self.ring, self.ring)
-        z = n // self.local + h * self.half
-        return (((z * self.ny + y) * self.nx + x) * self.nc + core) * self.local + n % self.local
-
-
-def collect(plan, rows, slot_pair, meta):
-    width, lanes = rows.shape[1:]
-    batch = plan.batch
-    steps = plan.ring * plan.rows
-
-    def kernel(sp, where, *refs):
+        self.rows = self.ring * self.ring
+
+    def bases(self):
+        x, y, core = (lax.axis_index(a).astype(jnp.int32) for a in ("x", "y", "core"))
+        entry = jnp.arange(4 * self.rows, dtype=jnp.int32)
+        h = entry % 2
+        t = (entry // 2) % self.ring
+        s = (entry // (2 * self.ring)) % self.ring
+        side = jnp.where(entry < 2 * self.rows, core, 1 - core)
+        py = (y - jnp.where(h == 0, s, t) + self.ring) % self.ring
+        px = (x - jnp.where(h == 0, t, s) + self.ring) % self.ring
+        return (((h * self.half * self.ny + py) * self.nx + px) * self.nc + side) * self.local
+
+    def offset(self, n):
+        return n // self.local * (self.ny * self.nx * self.nc * self.local) + n % self.local
+
+    def row_spec(self, n, first, tail):
+        h, n = n // self.batch, n % self.batch
+
+        def where_is(g, sp, base, *_):
+            return sp[base[first + 2 * g + h] + self.offset(n)], 0, 0
+
+        return pl.BlockSpec((1, *tail), where_is)
+
+
+def collect(plan, rows, slot_pair, bases):
+    tail = rows.shape[1:]
+    both = 2 * plan.batch
+
+    def kernel(sp, base, *refs):
         out = refs[-1]
-        for n in range(batch):
+        for n in range(both):
             out[n] = refs[n][0]
-
-    def spec(n):
-        def where_is(g, sp, where):
-            return sp[plan.slot(g // plan.rows, g % plan.rows, n, where, 1 - where[3])], 0, 0
-
-        return pl.BlockSpec((1, width, lanes), where_is)
 
     return pl.pallas_call(
         kernel,
         grid_spec=pltpu.PrefetchScalarGridSpec(
             num_scalar_prefetch=2,
-            grid=(steps,),
-            in_specs=[spec(n) for n in range(batch)],
-            out_specs=pl.BlockSpec((batch, width, lanes), lambda g, sp, where: (g, 0, 0)),
+            grid=(plan.rows,),
+            in_specs=[plan.row_spec(n, 2 * plan.rows, tail) for n in range(both)],
+            out_specs=pl.BlockSpec((both, *tail), lambda g, *_: (g, 0, 0)),
         ),
-        out_shape=jax.ShapeDtypeStruct((steps * batch, width, lanes), rows.dtype),
+        out_shape=jax.ShapeDtypeStruct((plan.rows * both, *tail), rows.dtype),
         cost_estimate=pl.CostEstimate(
-            flops=steps * batch * 10**6, bytes_accessed=steps * batch * 32768, transcendentals=0
+            flops=plan.rows * both * 10**6,
+            bytes_accessed=plan.rows * both * 32768,
+            transcendentals=0,
         ),
         name="collect",
-    )(slot_pair, meta, *([rows] * batch))
+    )(slot_pair, bases, *([rows] * both))
 
 
 def assemble(plan, column, parts):
@@ -83,27 +91,21 @@
     return pl.pallas_call(kernel, out_shape=(shape, shape), name="assemble")(column, *parts)
 
 
-def contract(plan, s, rows, sibling, amps, slot_pair, meta):
+def contract(plan, s, rows, sibling, amps, slot_pair, bases, token):
     width, lanes = rows.shape[1], rows.shape[2]
     side = width // 2
     batch, ring = plan.batch, plan.ring
 
-    def kernel(sp, where, *refs):
-        own, (sib, amp_0, amp_1, out_0, out_1, token, wide, held) = refs[:batch], refs[batch:]
-        g = pl.program_id(0)
+    both = 2 * batch
+
+    def kernel(sp, base_of, mark, *refs):
+        own, (sib, amp_0, amp_1, out_0, out_1, passed, wide) = refs[:both], refs[both:]
         low = lax.broadcasted_iota(jnp.int32, (side, lanes), 1) < lanes // 2
         zero = jnp.zeros((width, lanes), BF16)
         none = jnp.zeros((side, lanes), F32)
 
-        @pl.when(g < ring)
-        def _():
-            held[...] = amp_0[...]
-
-        @pl.when(g >= ring)
-        def _():
-            held[...] = amp_1[...]
-
-        for n in range(batch):
+        for n in range(both):
+            amp, out = (amp_0, out_0) if n < batch else (amp_1, out_1)
             base = n * 2 * width
             wide[pl.ds(base, width), :] = own[n][0].astype(F32)
             wide[pl.ds(base + width, width), :] = sib[n].astype(F32)
@@ -111,7 +113,7 @@
                 wide[pl.ds(base + u * width + p, side, stride=2), :] for u in range(2) for p in range(2)
             ]
             left = jnp.concatenate(parts, axis=0).astype(BF16)
-            amp_n = held[n]
+            amp_n = amp[n % batch]
             right = jnp.concatenate(
                 [
                     jnp.concatenate([amp_n, zero], axis=1),
@@ -148,54 +150,38 @@
                     ).astype(BF16)
                 )
             rhs = jnp.concatenate(cols, axis=1)
-            held[n] = lax.dot_general(
+            out[n % batch] = lax.dot_general(
                 lhs, rhs, (((1,), (1,)), ((), ())), preferred_element_type=F32
             ).astype(BF16)
 
-        @pl.when(g < ring)
-        def _():
-            out_0[...] = held[...]
-
-        @pl.when(g >= ring)
-        def _():
-            out_1[...] = held[...]
-
-        for i in range(4):
-            token[i] = where[i]
-
-    def own_spec(n):
-        def where_is(g, sp, where):
-            return sp[plan.slot(s, g, n, where, where[3])], 0, 0
-
-        return pl.BlockSpec((1, width, lanes), where_is)
+        passed[0] = mark[0]
 
     block = (batch, width, lanes)
-    first = pl.BlockSpec(block, lambda g, sp, where: (jnp.minimum(g, ring - 1), 0, 0))
-    second = pl.BlockSpec(block, lambda g, sp, where: (jnp.maximum(g - ring, 0), 0, 0))
+    own_half = pl.BlockSpec(block, lambda g, *_: (g, 0, 0))
     count = ring * batch
     shape = jax.ShapeDtypeStruct((count, width, lanes), BF16)
     return pl.pallas_call(
         kernel,
         grid_spec=pltpu.PrefetchScalarGridSpec(
-            num_scalar_prefetch=2,
-            grid=(plan.rows,),
-            in_specs=[own_spec(n) for n in range(batch)]
+            num_scalar_prefetch=3,
+            grid=(ring,),
+            in_specs=[plan.row_spec(n, 2 * s * ring, (width, lanes)) for n in range(both)]
             + [
-                pl.BlockSpec(block, lambda g, sp, where: (s * plan.rows + g, 0, 0)),
-                first,
-                second,
+                pl.BlockSpec((both, width, lanes), lambda g, *_: (s * ring + g, 0, 0)),
+                own_half,
+                own_half,
             ],
-            out_specs=(first, second, pl.BlockSpec(memory_space=pltpu.SMEM)),
-            scratch_shapes=[pltpu.VMEM((batch * 2 * width, lanes), F32), pltpu.VMEM(block, BF16)],
+            out_specs=(own_half, own_half, pl.BlockSpec(memory_space=pltpu.SMEM)),
+            scratch_shapes=[pltpu.VMEM((both * 2 * width, lanes), F32)],
         ),
-        out_shape=(shape, shape, jax.ShapeDtypeStruct((4,), jnp.int32)),
+        out_shape=(shape, shape, jax.ShapeDtypeStruct((1,), jnp.int32)),
         cost_estimate=pl.CostEstimate(
             flops=2 * count * 4 * (128 * 128 * 256),
             bytes_accessed=2 * count * 65536,
             transcendentals=0,
         ),
         name="contract",
-    )(slot_pair, meta, *([rows] * batch), sibling, *amps)
+    )(slot_pair, bases, token, *([rows] * both), sibling, *amps)
 
 
 def finish(line, amps, denom, square):
@@ -252,7 +238,7 @@
     local = amplitudes.shape[0]
     lanes = 2 * width
     plan = Plan(tuple(lax.axis_size(a) for a in AXES), local)
-    meta = jnp.stack([lax.axis_index(a) for a in AXES]).astype(jnp.int32)
+    bases = plan.bases()
 
     positions = jnp.arange(width, dtype=jnp.int32)
     masks = (positions[None, :] < ranks[:, None]).astype(F32)
@@ -276,20 +262,20 @@
     )
     column = column.reshape(nz * local, width, lanes)
 
-    sent = collect(plan, rows, slot_pair, meta)
+    sent = collect(plan, rows, slot_pair, bases)
     sibling = moved(sent, "core", 1)
 
     short, long = ("x", "y"), ("y", "x")
     pieces = [column[h * plan.batch : (h + 1) * plan.batch] for h in range(2)]
     parts = [moved(pieces[h], short[h], t) for h in range(2) for t in range(1, ring)]
     planes = assemble(plan, column, parts)
-    arrived = [planes] + [
-        tuple(moved(planes[h], long[h], s) for h in range(2)) for s in range(1, ring)
-    ]
+    arrived = [planes]
+    for s in range(1, ring):
+        arrived.append(tuple(moved(planes[h], long[h], s) for h in range(2)))
     back = [[], []]
-    token = meta
+    token = bases[:1]
     for s in range(ring):
-        *partial, token = contract(plan, s, rows, sibling, arrived[s], slot_pair, token)
+        *partial, token = contract(plan, s, rows, sibling, arrived[s], slot_pair, bases, token)
         for h in range(2):
             back[h].append(moved(partial[h], long[h], -s) if s else partial[h])
     halves = []

time: 248 us -> 234 us (0.944)
  Pallas kernels: 91.5 us -> 79.5 us
    pallas_call x1, Pallas kernels: 20.1 us -> 12.6 us  [collect(): pl.pallas_call(kernel, grid_spec=pltpu.PrefetchScalarGridSpec(num_scalar_...]
    pallas_call x4, Pallas kernels: 66.2 us -> 61.7 us  [contract(): pl.pallas_call(kernel, grid_spec=pltpu.PrefetchScalarGridSpec(num_scalar_...]
    unnamed x47 -> x45, local copies, waits for them, and re-layouts: 5.41 us -> 3.08 us
where the time goes in v1:
time: 234 us; the launch traced here: 231 us
  Pallas kernels  79.5 us (34%)
  waiting for transfers between devices  69 us (29%)
  starting transfers between devices  49.1 us (21%)
  blocking collectives  23.6 us (10%)
  local copies, waits for them, and re-layouts  4.47 us (2%)
  other arithmetic  3.8 us (2%)
    pallas_call x4, Pallas kernels, contract(): pl.pallas_call(kernel, grid_spec=pltpu.PrefetchScalarGridSpec(num_scalar_...  61.7 us
    ppermute x25, waiting for transfers between devices, moved(): return lax.ppermute(value, axis, [(j, (j + step) % n) for j in range(n)])  59.1 us
    ppermute x25, starting transfers between devices, moved(): return lax.ppermute(value, axis, [(j, (j + step) % n) for j in range(n)])  40.5 us
    all_to_all x1, blocking collectives, body(): lax.all_to_all(jnp.broadcast_to(mine, (nz, *mine.shape)), 'z', split_axis...  23.6 us
    pallas_call x1, Pallas kernels, collect(): pl.pallas_call(kernel, grid_spec=pltpu.PrefetchScalarGridSpec(num_scalar_...  12.6 us
    all_to_all x1, waiting for transfers between devices, body(): line = lax.all_to_all(line, 'z', split_axis=0, concat_axis=0, tiled=True)  9.85 us
    all_to_all x1, starting transfers between devices, body(): line = lax.all_to_all(line, 'z', split_axis=0, concat_axis=0, tiled=True)  8.67 us
  transfers between devices with their start and end apart: 26, of which 11 were waited for; matrix products, arithmetic and copies ran while one was open for 2% of the time, Pallas kernels for 21%

profile of v1, /device:TPU:24, one launch (start us, length us, event | category | flops | bytes accessed | tf_op | source)
XLA Modules:
  0.0 230.6 jit_solution(13030214613432821278)
XLA Ops:
  0.7 0.5 fusion.15.base.base_of
  1.2 12.6 %collect.1 = bf16[384,64,128]{2,1,0:T(8,128)(2,1)} custom-call(s32[768]{0:T(1024)} %sp.9, s32[64]{0:T(128)} %fusion.15.base.base_of, bf16[768,64,128]{2,1,0:T(8,128)(2,1)} %bitcast.56, bf16[768,64,128]{2,1,0:T(8,128)(2,1)} %bitcast.34, bf16[768,64,128]{2,1,0:T(8,128)(2,1)} %bitcast.35, bf16[768,64,128]{2,1,0:T(8,128)(2,1)} %bitcast.36, ...), custom_call_target="tpu_custom_call" | custom-call | flops 384000000 | bytes 12582912 | tf_op jit(solution)/shard_map/collect/pallas_call | solution.py:61
  14.2 0.6 copy-done.3
  15.2 23.6 %all_to_all.10 = bf16[8,3,64,128]{3,2,1,0:T(8,128)(2,1)S(1)} all-to-all(bf16[8,3,64,128]{3,2,1,0:T(8,128)(2,1)S(1)} %broadcast_in_dim.12), channel_id=1, replica_groups=mesh['z'=8,'y'=4,'x'=4,'core'=2] {'z'}, dimensions={0} | all-to-all | bytes 786432 | tf_op jit(solution)/shard_map/all_to_all | solution.py:260
  38.8 1.6 collective-permute-start.1
  40.4 2.7 %collective-permute-start.2 = (bf16[12,64,128]{2,1,0:T(8,128)(2,1)S(1)}, bf16[12,64,128]{2,1,0:T(8,128)(2,1)S(1)}, u32[]{:S(2)}, u32[]{:S(2)}) collective-permute-start(bf16[12,64,128]{2,1,0:T(8,128)(2,1)S(1)} %bitcast.158), channel_id=1, source_target_pairs={{0,4},{2,6},{4,0},{6,2},{1,5},{3,7},{5,1},{7,3},{8,12},{10,14},{12... | collective-permute-start | bytes 589832 | tf_op jit(solution)/shard_map/ppermute | solution.py:16
  43.1 1.4 collective-permute-start.3
  44.8 2.2 collective-permute-done.1.refs_0_
  47.0 1.2 collective-permute-start.5
  48.2 4.0 %collective-permute-done.2.refs_1_ = bf16[12,64,128]{2,1,0:T(8,128)(2,1)S(1)} collective-permute-done((bf16[12,64,128]{2,1,0:T(8,128)(2,1)S(1)}, bf16[12,64,128]{2,1,0:T(8,128)(2,1)S(1)}, u32[]{:S(2)}, u32[]{:S(2)}) %collective-permute-start.2) | collective-permute-done | bytes 196640 | tf_op jit(solution)/shard_map/ppermute | solution.py:16
  52.2 0.7 collective-permute-start.6
  52.9 2.4 %collective-permute-done.5.refs_4_ = bf16[12,64,128]{2,1,0:T(8,128)(2,1)S(1)} collective-permute-done((bf16[12,64,128]{2,1,0:T(8,128)(2,1)S(1)}, bf16[12,64,128]{2,1,0:T(8,128)(2,1)S(1)}, u32[]{:S(2)}, u32[]{:S(2)}) %collective-permute-start.5) | collective-permute-done | bytes 196640 | tf_op jit(solution)/shard_map/ppermute | solution.py:16
  55.3 4.1 %collective-permute-done.6.refs_5_ = bf16[12,64,128]{2,1,0:T(8,128)(2,1)S(1)} collective-permute-done((bf16[12,64,128]{2,1,0:T(8,128)(2,1)S(1)}, bf16[12,64,128]{2,1,0:T(8,128)(2,1)S(1)}, u32[]{:S(2)}, u32[]{:S(2)}) %collective-permute-start.6) | collective-permute-done | bytes 196640 | tf_op jit(solution)/shard_map/ppermute | solution.py:16
  59.5 0.6 copy-done.14
  60.1 2.6 %assemble.1 = (bf16[48,64,128]{2,1,0:T(8,128)(2,1)}, bf16[48,64,128]{2,1,0:T(8,128)(2,1)}) custom-call(bf16[24,64,128]{2,1,0:T(8,128)(2,1)} %bitcast.153, bf16[12,64,128]{2,1,0:T(8,128)(2,1)} %copy-done.9, bf16[12,64,128]{2,1,0:T(8,128)(2,1)} %copy-done.10, bf16[12,64,128]{2,1,0:T(8,128)(2,1)} %copy-done.11, bf16[12,64,128]{2,1,0:T(8,128)(2,1)} %copy-done.12, ...), custom_call_target="tpu_custom_call" | custom-call | tf_op jit(solution)/shard_map/assemble/pallas_call | solution.py:91
  62.8 1.4 collective-permute-start.10
  64.3 2.5 %collective-permute-start.11 = (bf16[48,64,128]{2,1,0:T(8,128)(2,1)}, bf16[48,64,128]{2,1,0:T(8,128)(2,1)}, u32[]{:S(2)}, u32[]{:S(2)}) collective-permute-start(bf16[48,64,128]{2,1,0:T(8,128)(2,1)} %get-tuple-element.18.refs_26_), channel_id=1, source_target_pairs={{0,4},{2,6},{4,0},{6,2},{1,5},{3,7},{5,1},{7,3},{8,12},{10,14},{12... | collective-permute-start | bytes 2359304 | tf_op jit(solution)/shard_map/ppermute | solution.py:16
  66.8 16.6 %collective-permute-done.7.refs_25_ = bf16[48,64,128]{2,1,0:T(8,128)(2,1)S(1)} collective-permute-done((bf16[48,64,128]{2,1,0:T(8,128)(2,1)}, bf16[48,64,128]{2,1,0:T(8,128)(2,1)S(1)}, u32[]{:S(2)}, u32[]{:S(2)}) %collective-permute-start.7) | collective-permute-done | bytes 786464 | tf_op jit(solution)/shard_map/ppermute | solution.py:16
  83.4 1.0 collective-permute-start.14
  84.4 15.4 %contract.4 = (bf16[48,64,128]{2,1,0:T(8,128)(2,1)}, bf16[48,64,128]{2,1,0:T(8,128)(2,1)}, s32[1]{0:T(128)}) custom-call(s32[768]{0:T(1024)} %sp.9, s32[64]{0:T(128)} %fusion.15.base.base_of, s32[1]{0:T(128)} %bitcast.161, bf16[768,64,128]{2,1,0:T(8,128)(2,1)} %bitcast.57, bf16[768,64,128]{2,1,0:T(8,128)(2,1)} %bitcast.58, bf16[768,64,128]{2,1,0:T(8,128)(2,1)} %bitcast.59, ...), custom_call_target="tpu_custom_call" | custom-call | flops 1610612736 | bytes 6291456 | tf_op jit(solution)/shard_map/contract/pallas_call | solution.py:163
  99.8 0.9 copy-done.6
  100.7 15.3 %contract.5 = (bf16[48,64,128]{2,1,0:T(8,128)(2,1)}, bf16[48,64,128]{2,1,0:T(8,128)(2,1)}, s32[1]{0:T(128)}) custom-call(s32[768]{0:T(1024)} %sp.9, s32[64]{0:T(128)} %fusion.15.base.base_of, s32[1]{0:T(128)} %get-tuple-element.20.mark, bf16[768,64,128]{2,1,0:T(8,128)(2,1)} %bitcast.92, bf16[768,64,128]{2,1,0:T(8,128)(2,1)} %bitcast.82, ...), custom_call_target="tpu_custom_call" | custom-call | flops 1610612736 | bytes 6291456 | tf_op jit(solution)/shard_map/contract/pallas_call | solution.py:163
  116.1 15.4 %contract.6 = (bf16[48,64,128]{2,1,0:T(8,128)(2,1)}, bf16[48,64,128]{2,1,0:T(8,128)(2,1)}, s32[1]{0:T(128)}) custom-call(s32[768]{0:T(1024)} %sp.9, s32[64]{0:T(128)} %fusion.15.base.base_of, s32[1]{0:T(128)} %get-tuple-element.22.mark, bf16[768,64,128]{2,1,0:T(8,128)(2,1)} %bitcast.117, bf16[768,64,128]{2,1,0:T(8,128)(2,1)} %bitcast.106, ...), custom_call_target="tpu_custom_call" | custom-call | flops 1610612736 | bytes 6291456 | tf_op jit(solution)/shard_map/contract/pallas_call | solution.py:163
  131.5 15.6 %contract.7 = (bf16[48,64,128]{2,1,0:T(8,128)(2,1)}, bf16[48,64,128]{2,1,0:T(8,128)(2,1)}, s32[1]{0:T(128)}) custom-call(s32[768]{0:T(1024)} %sp.9, s32[64]{0:T(128)} %fusion.15.base.base_of, s32[1]{0:T(128)} %get-tuple-element.24.mark, bf16[768,64,128]{2,1,0:T(8,128)(2,1)} %bitcast.129, bf16[768,64,128]{2,1,0:T(8,128)(2,1)} %bitcast.130, ...), custom_call_target="tpu_custom_call" | custom-call | flops 1610612736 | bytes 6291456 | tf_op jit(solution)/shard_map/contract/pallas_call | solution.py:163
  147.2 1.3 collective-permute-start.21
  148.5 2.2 collective-permute-start.20
  150.7 0.6 collective-permute-start.19
  151.4 3.0 %collective-permute-start.15 = (bf16[48,64,128]{2,1,0:T(8,128)(2,1)}, bf16[48,64,128]{2,1,0:T(8,128)(2,1)S(1)}, u32[]{:S(2)}, u32[]{:S(2)}) collective-permute-start(bf16[48,64,128]{2,1,0:T(8,128)(2,1)} %get-tuple-element.25), channel_id=1, source_target_pairs={{0,8},{8,16},{16,24},{24,0},{1,9},{9,17},{17,25},{25,1},{2,10},{10... | collective-permute-start | bytes 2359304 | tf_op jit(solution)/shard_map/ppermute | solution.py:16
  154.6 12.4 %collective-permute-done.21 = bf16[48,64,128]{2,1,0:T(8,128)(2,1)S(1)} collective-permute-done((bf16[48,64,128]{2,1,0:T(8,128)(2,1)}, bf16[48,64,128]{2,1,0:T(8,128)(2,1)S(1)}, u32[]{:S(2)}, u32[]{:S(2)}) %collective-permute-start.21) | collective-permute-done | bytes 786464 | tf_op jit(solution)/shard_map/ppermute | solution.py:16
  167.0 1.3 collective-permute-start.9
  168.3 13.4 %collective-permute-done.20 = bf16[48,64,128]{2,1,0:T(8,128)(2,1)S(1)} collective-permute-done((bf16[48,64,128]{2,1,0:T(8,128)(2,1)}, bf16[48,64,128]{2,1,0:T(8,128)(2,1)S(1)}, u32[]{:S(2)}, u32[]{:S(2)}) %collective-permute-start.20) | collective-permute-done | bytes 786464 | tf_op jit(solution)/shard_map/ppermute | solution.py:16
  181.6 0.6 add_convert_fusion
  182.3 2.8 %collective-permute-start.24 = (bf16[12,64,128]{2,1,0:T(8,128)(2,1)S(1)}, bf16[12,64,128]{2,1,0:T(8,128)(2,1)S(1)}, u32[]{:S(2)}, u32[]{:S(2)}) collective-permute-start(bf16[12,64,128]{2,1,0:T(8,128)(2,1)S(1)} %get-tuple-element.36), channel_id=1, source_target_pairs={{0,8},{8,16},{16,24},{24,0},{1,9},{9,17},{17,25},{25,1},{2,10},{10... | collective-permute-start | bytes 589832 | tf_op jit(solution)/shard_map/ppermute | solution.py:16
  185.1 0.3 collective-permute-start.23
  185.4 1.0 collective-permute-start.22
  186.4 1.0 collective-permute-done.9
  187.5 0.6 add_convert_fusion.1
  188.1 9.6 %collective-permute-start.18 = (bf16[12,64,128]{2,1,0:T(8,128)(2,1)S(1)}, bf16[12,64,128]{2,1,0:T(8,128)(2,1)S(1)}, u32[]{:S(2)}, u32[]{:S(2)}) collective-permute-start(bf16[12,64,128]{2,1,0:T(8,128)(2,1)S(1)} %get-tuple-element.33), channel_id=1, source_target_pairs={{0,2},{2,4},{4,6},{6,0},{1,3},{3,5},{5,7},{7,1},{8,10},{10,12},{12... | collective-permute-start | bytes 589832 | tf_op jit(solution)/shard_map/ppermute | solution.py:16
  197.7 2.5 %collective-permute-start.17 = (bf16[12,64,128]{2,1,0:T(8,128)(2,1)S(1)}, bf16[12,64,128]{2,1,0:T(8,128)(2,1)S(1)}, u32[]{:S(2)}, u32[]{:S(2)}) collective-permute-start(bf16[12,64,128]{2,1,0:T(8,128)(2,1)S(1)} %get-tuple-element.34), channel_id=1, source_target_pairs={{0,4},{2,6},{4,0},{6,2},{1,5},{3,7},{5,1},{7,3},{8,12},{10,14},{12... | collective-permute-start | bytes 589832 | tf_op jit(solution)/shard_map/ppermute | solution.py:16
  200.2 2.5 %collective-permute-start.16 = (bf16[12,64,128]{2,1,0:T(8,128)(2,1)S(1)}, bf16[12,64,128]{2,1,0:T(8,128)(2,1)S(1)}, u32[]{:S(2)}, u32[]{:S(2)}) collective-permute-start(bf16[12,64,128]{2,1,0:T(8,128)(2,1)S(1)} %get-tuple-element.32), channel_id=1, source_target_pairs={{0,6},{2,0},{4,2},{6,4},{1,7},{3,1},{5,3},{7,5},{8,14},{10,8},{12,... | collective-permute-start | bytes 589832 | tf_op jit(solution)/shard_map/ppermute | solution.py:16
  202.9 3.0 %collective-permute-done.17 = bf16[12,64,128]{2,1,0:T(8,128)(2,1)S(1)} collective-permute-done((bf16[12,64,128]{2,1,0:T(8,128)(2,1)S(1)}, bf16[12,64,128]{2,1,0:T(8,128)(2,1)S(1)}, u32[]{:S(2)}, u32[]{:S(2)}) %collective-permute-start.17) | collective-permute-done | bytes 196640 | tf_op jit(solution)/shard_map/ppermute | solution.py:16
  206.0 0.8 pad_maximum_fusion
  206.8 8.7 %all-to-all-start.1 = ((bf16[8,3,64,128]{3,2,1,0:T(8,128)(2,1)}), bf16[8,3,64,128]{3,2,1,0:T(8,128)(2,1)S(1)}, u32[]{:S(2)}, u32[]{:S(2)}) async-start(bf16[8,3,64,128]{3,2,1,0:T(8,128)(2,1)} %bitcast.9), calls=%async_computation.1 | async-start | bytes 786432 | tf_op jit(solution)/shard_map/all_to_all | solution.py:287
  215.6 0.7 mul.56.sq_ref
  216.8 0.7 broadcast_subtract_fusion.den_ref
  217.6 9.8 %all-to-all-done.1.line_ref = bf16[8,3,64,128]{3,2,1,0:T(8,128)(2,1)S(1)} async-done(((bf16[8,3,64,128]{3,2,1,0:T(8,128)(2,1)}), bf16[8,3,64,128]{3,2,1,0:T(8,128)(2,1)S(1)}, u32[]{:S(2)}, u32[]{:S(2)}) %all-to-all-start.1) | async-done | bytes 393248 | tf_op jit(solution)/shard_map/all_to_all | solution.py:287
  227.4 0.8 copy-done.2
  228.2 2.5 %finish.1 = (f32[3,64,128]{2,1,0:T(8,128)}, bf16[3,64,128]{2,1,0:T(8,128)(2,1)}) custom-call(bf16[8,3,64,128]{3,2,1,0:T(8,128)(2,1)} %copy-done.2, bf16[3,64,128]{2,1,0:T(8,128)(2,1)} %bitcast.160, f32[3,32,128]{2,1,0:T(8,128)} %broadcast_subtract_fusion.den_ref, f32[3,32,128]{2,1,0:T(8,128)} %mul.56.sq_ref), custom_call_target="tpu_custom_call" | custom-call | tf_op jit(solution)/shard_map/finish/pallas_call | solution.py:221
  (80 shorter events, 2.3 us)
Async XLA Ops:
  0.6 215.9 %copy-start = (f32[48]{0:T(128)S(1)}, f32[48]{0:T(128)}, u32[]{:S(2)}) copy-start(f32[48]{0:T(128)} %param.13) | copy-start | bytes 580
  1.2 12.7 %copy-start.15 = (bf16[3,2,4096]{2,1,0:T(2,128)(2,1)S(1)}, bf16[3,2,4096]{2,1,0:T(2,128)(2,1)}, u32[]{:S(2)}) copy-start(bf16[3,2,4096]{2,1,0:T(2,128)(2,1)} %param.9) | copy-start | bytes 147460
  1.2 12.9 %copy-start.18 = (s32[3]{0:T(128)S(1)}, s32[3]{0:T(128)}, u32[]{:S(2)}) copy-start(s32[3]{0:T(128)} %param.10) | copy-start | bytes 40
  13.8 69.6 %collective-permute-start = (bf16[384,64,128]{2,1,0:T(8,128)(2,1)}, bf16[384,64,128]{2,1,0:T(8,128)(2,1)}, u32[]{:S(2)}, u32[]{:S(2)}) collective-permute-start(bf16[384,64,128]{2,1,0:T(8,128)(2,1)} %collect.1), channel_id=1, source_target_pairs={{0,1},{1,0},{2,3},{3,2},{4,5},{5,4},{6,7},{7,6},{8,9},{9,8},{10,11... | collective-permute-start | bytes 18874376 | tf_op jit(solution)/shard_map/ppermute | solution.py:16
  14.2 0.6 copy-start.3
  38.8 20.7 %copy-start.1 = (bf16[8,3,64,128]{3,2,1,0:T(8,128)(2,1)}, bf16[8,3,64,128]{3,2,1,0:T(8,128)(2,1)S(1)}, u32[]{:S(2)}) copy-start(bf16[8,3,64,128]{3,2,1,0:T(8,128)(2,1)S(1)} %all_to_all.10) | copy-start | bytes 1179652
  38.8 8.1 %collective-permute-start.1 = (bf16[12,64,128]{2,1,0:T(8,128)(2,1)S(1)}, bf16[12,64,128]{2,1,0:T(8,128)(2,1)S(1)}, u32[]{:S(2)}, u32[]{:S(2)}) collective-permute-start(bf16[12,64,128]{2,1,0:T(8,128)(2,1)S(1)} %bitcast.157), channel_id=1, source_target_pairs={{0,2},{2,4},{4,6},{6,0},{1,3},{3,5},{5,7},{7,1},{8,10},{10,12},{12... | collective-permute-start | bytes 589832 | tf_op jit(solution)/shard_map/ppermute | solution.py:16
  40.4 11.8 %collective-permute-start.2 = (bf16[12,64,128]{2,1,0:T(8,128)(2,1)S(1)}, bf16[12,64,128]{2,1,0:T(8,128)(2,1)S(1)}, u32[]{:S(2)}, u32[]{:S(2)}) collective-permute-start(bf16[12,64,128]{2,1,0:T(8,128)(2,1)S(1)} %bitcast.158), channel_id=1, source_target_pairs={{0,4},{2,6},{4,0},{6,2},{1,5},{3,7},{5,1},{7,3},{8,12},{10,14},{12... | collective-permute-start | bytes 589832 | tf_op jit(solution)/shard_map/ppermute | solution.py:16
  43.1 9.8 %collective-permute-start.3 = (bf16[12,64,128]{2,1,0:T(8,128)(2,1)S(1)}, bf16[12,64,128]{2,1,0:T(8,128)(2,1)S(1)}, u32[]{:S(2)}, u32[]{:S(2)}) collective-permute-start(bf16[12,64,128]{2,1,0:T(8,128)(2,1)S(1)} %bitcast.159), channel_id=1, source_target_pairs={{0,6},{2,0},{4,2},{6,4},{1,7},{3,1},{5,3},{7,5},{8,14},{10,8},{12,... | collective-permute-start | bytes 589832 | tf_op jit(solution)/shard_map/ppermute | solution.py:16
  44.6 8.4 %collective-permute-start.4 = (bf16[12,64,128]{2,1,0:T(8,128)(2,1)S(1)}, bf16[12,64,128]{2,1,0:T(8,128)(2,1)S(1)}, u32[]{:S(2)}, u32[]{:S(2)}) collective-permute-start(bf16[12,64,128]{2,1,0:T(8,128)(2,1)S(1)} %bitcast.154), channel_id=1, source_target_pairs={{0,8},{8,16},{16,24},{24,0},{1,9},{9,17},{17,25},{25,1},{2,10},{10... | collective-permute-start | bytes 589832 | tf_op jit(solution)/shard_map/ppermute | solution.py:16
  47.0 12.5 %copy-start.9 = (bf16[12,64,128]{2,1,0:T(8,128)(2,1)}, bf16[12,64,128]{2,1,0:T(8,128)(2,1)S(1)}, u32[]{:S(2)}) copy-start(bf16[12,64,128]{2,1,0:T(8,128)(2,1)S(1)} %collective-permute-done.1.refs_0_) | copy-start | bytes 589828
  47.0 8.4 %collective-permute-start.5 = (bf16[12,64,128]{2,1,0:T(8,128)(2,1)S(1)}, bf16[12,64,128]{2,1,0:T(8,128)(2,1)S(1)}, u32[]{:S(2)}, u32[]{:S(2)}) collective-permute-start(bf16[12,64,128]{2,1,0:T(8,128)(2,1)S(1)} %bitcast.155), channel_id=1, source_target_pairs={{0,16},{8,24},{16,0},{24,8},{1,17},{9,25},{17,1},{25,9},{2,18},{10... | collective-permute-start | bytes 589832 | tf_op jit(solution)/shard_map/ppermute | solution.py:16
  52.2 7.3 %copy-start.10 = (bf16[12,64,128]{2,1,0:T(8,128)(2,1)}, bf16[12,64,128]{2,1,0:T(8,128)(2,1)S(1)}, u32[]{:S(2)}) copy-start(bf16[12,64,128]{2,1,0:T(8,128)(2,1)S(1)} %collective-permute-done.2.refs_1_) | copy-start | bytes 589828
  52.2 7.3 %collective-permute-start.6 = (bf16[12,64,128]{2,1,0:T(8,128)(2,1)S(1)}, bf16[12,64,128]{2,1,0:T(8,128)(2,1)S(1)}, u32[]{:S(2)}, u32[]{:S(2)}) collective-permute-start(bf16[12,64,128]{2,1,0:T(8,128)(2,1)S(1)} %bitcast.156), channel_id=1, source_target_pairs={{0,24},{8,0},{16,8},{24,16},{1,25},{9,1},{17,9},{25,17},{2,26},{10... | collective-permute-start | bytes 589832 | tf_op jit(solution)/shard_map/ppermute | solution.py:16
  52.9 6.6 %copy-start.11 = (bf16[12,64,128]{2,1,0:T(8,128)(2,1)}, bf16[12,64,128]{2,1,0:T(8,128)(2,1)S(1)}, u32[]{:S(2)}) copy-start(bf16[12,64,128]{2,1,0:T(8,128)(2,1)S(1)} %collective-permute-done.3.refs_2_) | copy-start | bytes 589828
  52.9 6.6 %copy-start.12 = (bf16[12,64,128]{2,1,0:T(8,128)(2,1)}, bf16[12,64,128]{2,1,0:T(8,128)(2,1)S(1)}, u32[]{:S(2)}) copy-start(bf16[12,64,128]{2,1,0:T(8,128)(2,1)S(1)} %collective-permute-done.4.refs_3_) | copy-start | bytes 589828
  55.3 4.2 %copy-start.13 = (bf16[12,64,128]{2,1,0:T(8,128)(2,1)}, bf16[12,64,128]{2,1,0:T(8,128)(2,1)S(1)}, u32[]{:S(2)}) copy-start(bf16[12,64,128]{2,1,0:T(8,128)(2,1)S(1)} %collective-permute-done.5.refs_4_) | copy-start | bytes 589828
  59.5 0.7 copy-start.14
  62.8 20.6 %collective-permute-start.7 = (bf16[48,64,128]{2,1,0:T(8,128)(2,1)}, bf16[48,64,128]{2,1,0:T(8,128)(2,1)S(1)}, u32[]{:S(2)}, u32[]{:S(2)}) collective-permute-start(bf16[48,64,128]{2,1,0:T(8,128)(2,1)} %get-tuple-element.17.refs_25_), channel_id=1, source_target_pairs={{0,8},{8,16},{16,24},{24,0},{1,9},{9,17},{17,25},{25,1},{2,10},{10... | collective-permute-start | bytes 2359304 | tf_op jit(solution)/shard_map/ppermute | solution.py:16
  62.8 37.1 %collective-permute-start.8 = (bf16[48,64,128]{2,1,0:T(8,128)(2,1)}, bf16[48,64,128]{2,1,0:T(8,128)(2,1)S(1)}, u32[]{:S(2)}, u32[]{:S(2)}) collective-permute-start(bf16[48,64,128]{2,1,0:T(8,128)(2,1)} %get-tuple-element.18.refs_26_), channel_id=1, source_target_pairs={{0,2},{2,4},{4,6},{6,0},{1,3},{3,5},{5,7},{7,1},{8,10},{10,12},{12... | collective-permute-start | bytes 2359304 | tf_op jit(solution)/shard_map/ppermute | solution.py:16
  62.8 53.2 %collective-permute-start.10 = (bf16[48,64,128]{2,1,0:T(8,128)(2,1)}, bf16[48,64,128]{2,1,0:T(8,128)(2,1)}, u32[]{:S(2)}, u32[]{:S(2)}) collective-permute-start(bf16[48,64,128]{2,1,0:T(8,128)(2,1)} %get-tuple-element.17.refs_25_), channel_id=1, source_target_pairs={{0,16},{8,24},{16,0},{24,8},{1,17},{9,25},{17,1},{25,9},{2,18},{10... | collective-permute-start | bytes 2359304 | tf_op jit(solution)/shard_map/ppermute | solution.py:16
  64.3 51.8 %collective-permute-start.11 = (bf16[48,64,128]{2,1,0:T(8,128)(2,1)}, bf16[48,64,128]{2,1,0:T(8,128)(2,1)}, u32[]{:S(2)}, u32[]{:S(2)}) collective-permute-start(bf16[48,64,128]{2,1,0:T(8,128)(2,1)} %get-tuple-element.18.refs_26_), channel_id=1, source_target_pairs={{0,4},{2,6},{4,0},{6,2},{1,5},{3,7},{5,1},{7,3},{8,12},{10,14},{12... | collective-permute-start | bytes 2359304 | tf_op jit(solution)/shard_map/ppermute | solution.py:16
  83.4 16.4 %copy-start.5 = (bf16[48,64,128]{2,1,0:T(8,128)(2,1)}, bf16[48,64,128]{2,1,0:T(8,128)(2,1)S(1)}, u32[]{:S(2)}) copy-start(bf16[48,64,128]{2,1,0:T(8,128)(2,1)S(1)} %collective-permute-done.7.refs_25_) | copy-start | bytes 2359300
  83.4 48.1 %collective-permute-start.13 = (bf16[48,64,128]{2,1,0:T(8,128)(2,1)}, bf16[48,64,128]{2,1,0:T(8,128)(2,1)}, u32[]{:S(2)}, u32[]{:S(2)}) collective-permute-start(bf16[48,64,128]{2,1,0:T(8,128)(2,1)} %get-tuple-element.17.refs_25_), channel_id=1, source_target_pairs={{0,24},{8,0},{16,8},{24,16},{1,25},{9,1},{17,9},{25,17},{2,26},{10... | collective-permute-start | bytes 2359304 | tf_op jit(solution)/shard_map/ppermute | solution.py:16
  83.4 48.1 %collective-permute-start.14 = (bf16[48,64,128]{2,1,0:T(8,128)(2,1)}, bf16[48,64,128]{2,1,0:T(8,128)(2,1)}, u32[]{:S(2)}, u32[]{:S(2)}) collective-permute-start(bf16[48,64,128]{2,1,0:T(8,128)(2,1)} %get-tuple-element.18.refs_26_), channel_id=1, source_target_pairs={{0,6},{2,0},{4,2},{6,4},{1,7},{3,1},{5,3},{7,5},{8,14},{10,8},{12,... | collective-permute-start | bytes 2359304 | tf_op jit(solution)/shard_map/ppermute | solution.py:16
  99.8 0.9 copy-start.6
  131.5 19.2 %copy-start.21 = (bf16[48,64,128]{2,1,0:T(8,128)(2,1)S(1)}, bf16[48,64,128]{2,1,0:T(8,128)(2,1)}, u32[]{:S(2)}) copy-start(bf16[48,64,128]{2,1,0:T(8,128)(2,1)} %get-tuple-element.27) | copy-start | bytes 2359300
  131.5 22.8 %copy-start.20 = (bf16[48,64,128]{2,1,0:T(8,128)(2,1)S(1)}, bf16[48,64,128]{2,1,0:T(8,128)(2,1)}, u32[]{:S(2)}) copy-start(bf16[48,64,128]{2,1,0:T(8,128)(2,1)} %get-tuple-element.23) | copy-start | bytes 2359300
  131.5 35.5 %copy-start.19 = (bf16[48,64,128]{2,1,0:T(8,128)(2,1)S(1)}, bf16[48,64,128]{2,1,0:T(8,128)(2,1)}, u32[]{:S(2)}) copy-start(bf16[48,64,128]{2,1,0:T(8,128)(2,1)} %get-tuple-element.21) | copy-start | bytes 2359300
  131.5 50.1 %copy-start.8 = (bf16[48,64,128]{2,1,0:T(8,128)(2,1)S(1)}, bf16[48,64,128]{2,1,0:T(8,128)(2,1)}, u32[]{:S(2)}) copy-start(bf16[48,64,128]{2,1,0:T(8,128)(2,1)} %get-tuple-element.26) | copy-start | bytes 2359300
  147.2 19.8 %collective-permute-start.21 = (bf16[48,64,128]{2,1,0:T(8,128)(2,1)}, bf16[48,64,128]{2,1,0:T(8,128)(2,1)S(1)}, u32[]{:S(2)}, u32[]{:S(2)}) collective-permute-start(bf16[48,64,128]{2,1,0:T(8,128)(2,1)} %get-tuple-element.29), channel_id=1, source_target_pairs={{0,2},{2,4},{4,6},{6,0},{1,3},{3,5},{5,7},{7,1},{8,10},{10,12},{12... | collective-permute-start | bytes 2359304 | tf_op jit(solution)/shard_map/ppermute | solution.py:16
  148.5 33.1 %collective-permute-start.20 = (bf16[48,64,128]{2,1,0:T(8,128)(2,1)}, bf16[48,64,128]{2,1,0:T(8,128)(2,1)S(1)}, u32[]{:S(2)}, u32[]{:S(2)}) collective-permute-start(bf16[48,64,128]{2,1,0:T(8,128)(2,1)} %get-tuple-element.28), channel_id=1, source_target_pairs={{0,4},{2,6},{4,0},{6,2},{1,5},{3,7},{5,1},{7,3},{8,12},{10,14},{12... | collective-permute-start | bytes 2359304 | tf_op jit(solution)/shard_map/ppermute | solution.py:16
  150.7 30.9 %collective-permute-start.19 = (bf16[48,64,128]{2,1,0:T(8,128)(2,1)S(1)}, bf16[48,64,128]{2,1,0:T(8,128)(2,1)S(1)}, u32[]{:S(2)}, u32[]{:S(2)}) collective-permute-start(bf16[48,64,128]{2,1,0:T(8,128)(2,1)S(1)} %copy-done.21), channel_id=1, source_target_pairs={{0,6},{2,0},{4,2},{6,4},{1,7},{3,1},{5,3},{7,5},{8,14},{10,8},{12,... | collective-permute-start | bytes 2359304 | tf_op jit(solution)/shard_map/ppermute | solution.py:16
  151.4 34.0 %collective-permute-start.15 = (bf16[48,64,128]{2,1,0:T(8,128)(2,1)}, bf16[48,64,128]{2,1,0:T(8,128)(2,1)S(1)}, u32[]{:S(2)}, u32[]{:S(2)}) collective-permute-start(bf16[48,64,128]{2,1,0:T(8,128)(2,1)} %get-tuple-element.25), channel_id=1, source_target_pairs={{0,8},{8,16},{16,24},{24,0},{1,9},{9,17},{17,25},{25,1},{2,10},{10... | collective-permute-start | bytes 2359304 | tf_op jit(solution)/shard_map/ppermute | solution.py:16
  154.3 32.1 %collective-permute-start.12 = (bf16[48,64,128]{2,1,0:T(8,128)(2,1)S(1)}, bf16[48,64,128]{2,1,0:T(8,128)(2,1)S(1)}, u32[]{:S(2)}, u32[]{:S(2)}) collective-permute-start(bf16[48,64,128]{2,1,0:T(8,128)(2,1)S(1)} %copy-done.20), channel_id=1, source_target_pairs={{0,16},{8,24},{16,0},{24,8},{1,17},{9,25},{17,1},{25,9},{2,18},{10... | collective-permute-start | bytes 2359304 | tf_op jit(solution)/shard_map/ppermute | solution.py:16
  167.0 20.5 %collective-permute-start.9 = (bf16[48,64,128]{2,1,0:T(8,128)(2,1)S(1)}, bf16[48,64,128]{2,1,0:T(8,128)(2,1)S(1)}, u32[]{:S(2)}, u32[]{:S(2)}) collective-permute-start(bf16[48,64,128]{2,1,0:T(8,128)(2,1)S(1)} %copy-done.19), channel_id=1, source_target_pairs={{0,24},{8,0},{16,8},{24,16},{1,25},{9,1},{17,9},{25,17},{2,26},{10... | collective-permute-start | bytes 2359304 | tf_op jit(solution)/shard_map/ppermute | solution.py:16
  182.3 5.2 %copy-start.7 = (bf16[48,64,128]{2,1,0:T(8,128)(2,1)S(1)}, bf16[48,64,128]{2,1,0:T(8,128)(2,1)}, u32[]{:S(2)}) copy-start(bf16[48,64,128]{2,1,0:T(8,128)(2,1)} %get-tuple-element.19) | copy-start | bytes 2359300
  182.3 17.9 %collective-permute-start.24 = (bf16[12,64,128]{2,1,0:T(8,128)(2,1)S(1)}, bf16[12,64,128]{2,1,0:T(8,128)(2,1)S(1)}, u32[]{:S(2)}, u32[]{:S(2)}) collective-permute-start(bf16[12,64,128]{2,1,0:T(8,128)(2,1)S(1)} %get-tuple-element.36), channel_id=1, source_target_pairs={{0,8},{8,16},{16,24},{24,0},{1,9},{9,17},{17,25},{25,1},{2,10},{10... | collective-permute-start | bytes 589832 | tf_op jit(solution)/shard_map/ppermute | solution.py:16
  185.1 17.6 %collective-permute-start.23 = (bf16[12,64,128]{2,1,0:T(8,128)(2,1)S(1)}, bf16[12,64,128]{2,1,0:T(8,128)(2,1)S(1)}, u32[]{:S(2)}, u32[]{:S(2)}) collective-permute-start(bf16[12,64,128]{2,1,0:T(8,128)(2,1)S(1)} %get-tuple-element.37), channel_id=1, source_target_pairs={{0,16},{8,24},{16,0},{24,8},{1,17},{9,25},{17,1},{25,9},{2,18},{10... | collective-permute-start | bytes 589832 | tf_op jit(solution)/shard_map/ppermute | solution.py:16
  185.4 17.4 %collective-permute-start.22 = (bf16[12,64,128]{2,1,0:T(8,128)(2,1)S(1)}, bf16[12,64,128]{2,1,0:T(8,128)(2,1)S(1)}, u32[]{:S(2)}, u32[]{:S(2)}) collective-permute-start(bf16[12,64,128]{2,1,0:T(8,128)(2,1)S(1)} %get-tuple-element.35), channel_id=1, source_target_pairs={{0,24},{8,0},{16,8},{24,16},{1,25},{9,1},{17,9},{25,17},{2,26},{10... | collective-permute-start | bytes 589832 | tf_op jit(solution)/shard_map/ppermute | solution.py:16
  188.1 14.8 %collective-permute-start.18 = (bf16[12,64,128]{2,1,0:T(8,128)(2,1)S(1)}, bf16[12,64,128]{2,1,0:T(8,128)(2,1)S(1)}, u32[]{:S(2)}, u32[]{:S(2)}) collective-permute-start(bf16[12,64,128]{2,1,0:T(8,128)(2,1)S(1)} %get-tuple-element.33), channel_id=1, source_target_pairs={{0,2},{2,4},{4,6},{6,0},{1,3},{3,5},{5,7},{7,1},{8,10},{10,12},{12... | collective-permute-start | bytes 589832 | tf_op jit(solution)/shard_map/ppermute | solution.py:16
  197.7 8.1 %collective-permute-start.17 = (bf16[12,64,128]{2,1,0:T(8,128)(2,1)S(1)}, bf16[12,64,128]{2,1,0:T(8,128)(2,1)S(1)}, u32[]{:S(2)}, u32[]{:S(2)}) collective-permute-start(bf16[12,64,128]{2,1,0:T(8,128)(2,1)S(1)} %get-tuple-element.34), channel_id=1, source_target_pairs={{0,4},{2,6},{4,0},{6,2},{1,5},{3,7},{5,1},{7,3},{8,12},{10,14},{12... | collective-permute-start | bytes 589832 | tf_op jit(solution)/shard_map/ppermute | solution.py:16
  200.2 15.3 %copy-start.16 = (f32[3,64]{1,0:T(4,128)S(1)}, f32[3,64]{1,0:T(4,128)}, u32[]{:S(2)}) copy-start(f32[3,64]{1,0:T(4,128)} %param.12) | copy-start | bytes 2308
  200.2 5.7 %collective-permute-start.16 = (bf16[12,64,128]{2,1,0:T(8,128)(2,1)S(1)}, bf16[12,64,128]{2,1,0:T(8,128)(2,1)S(1)}, u32[]{:S(2)}, u32[]{:S(2)}) collective-permute-start(bf16[12,64,128]{2,1,0:T(8,128)(2,1)S(1)} %get-tuple-element.32), channel_id=1, source_target_pairs={{0,6},{2,0},{4,2},{6,4},{1,7},{3,1},{5,3},{7,5},{8,14},{10,8},{12,... | collective-permute-start | bytes 589832 | tf_op jit(solution)/shard_map/ppermute | solution.py:16
  202.9 12.8 %copy-start.4 = (f32[3,64,64]{2,1,0:T(8,128)S(1)}, f32[3,64,64]{2,1,0:T(8,128)}, u32[]{:S(2)}) copy-start(f32[3,64,64]{2,1,0:T(8,128)} %copy-done.3) | copy-start | bytes 147460
  202.9 13.5 %copy-start.17 = (s32[3,2]{0,1:T(2,128)S(1)}, s32[3,2]{0,1:T(2,128)}, u32[]{:S(2)}) copy-start(s32[3,2]{0,1:T(2,128)} %param.11) | copy-start | bytes 76
  206.8 20.6 %all-to-all-start.1 = ((bf16[8,3,64,128]{3,2,1,0:T(8,128)(2,1)}), bf16[8,3,64,128]{3,2,1,0:T(8,128)(2,1)S(1)}, u32[]{:S(2)}, u32[]{:S(2)}) async-start(bf16[8,3,64,128]{3,2,1,0:T(8,128)(2,1)} %bitcast.9), calls=%async_computation.1 | async-start | bytes 786432 | tf_op jit(solution)/shard_map/all_to_all | solution.py:287
  227.4 0.8 copy-start.2

commit v2 on v1

--- a/solution.py
+++ b/solution.py
@@ -14,6 +14,10 @@
 def moved(value, axis, step):
     n = lax.axis_size(axis)
     return lax.ppermute(value, axis, [(j, (j + step) % n) for j in range(n)])
+
+
+def step_order(ring):
+    return sorted(range(ring), key=lambda s: min(s, ring - s))
 
 
 class Plan:
@@ -102,7 +106,6 @@
         own, (sib, amp_0, amp_1, out_0, out_1, passed, wide) = refs[:both], refs[both:]
         low = lax.broadcasted_iota(jnp.int32, (side, lanes), 1) < lanes // 2
         zero = jnp.zeros((width, lanes), BF16)
-        none = jnp.zeros((side, lanes), F32)
 
         for n in range(both):
             amp, out = (amp_0, out_0) if n < batch else (amp_1, out_1)
@@ -121,37 +124,45 @@
                 ],
                 axis=0,
             )
-            inner_w = jnp.dot(left, right, preferred_element_type=F32).astype(BF16)
+            inner_w = jnp.dot(left, right, preferred_element_type=F32).astype(BF16).astype(F32)
+            turns = [pltpu.roll(part, lanes // 2, 1) for part in parts]
+            blocks = [
+                [inner_w[p * side : (p + 1) * side, u * lanes : (u + 1) * lanes] for u in range(2)]
+                for p in range(4)
+            ]
+            lhs, rhs = [[], []], []
+            for p in (0, 2):
+                rhs.append(
+                    jnp.concatenate(
+                        [
+                            jnp.where(low, parts[p], turns[p + 1]),
+                            jnp.where(low, turns[p], parts[p + 1]),
+                        ],
+                        axis=0,
+                    )
+                )
+                for u in range(2):
+                    even, odd = blocks[p][u], blocks[p + 1][u]
+                    lhs[u].append(
+                        (
+                            jnp.where(low, even, pltpu.roll(odd, lanes // 2, 1)),
+                            jnp.where(low, pltpu.roll(even, lanes // 2, 1), odd),
+                        )
+                    )
             lhs = jnp.concatenate(
                 [
-                    jnp.concatenate(
-                        [
-                            inner_w[p * side : (p + 1) * side, u * lanes : (u + 1) * lanes]
-                            for p in range(4)
-                        ],
-                        axis=1,
-                    )
+                    jnp.concatenate([lhs[u][q][k] for q in range(2)], axis=1)
+                    for k in range(2)
                     for u in range(2)
                 ],
                 axis=0,
+            ).astype(BF16)
+            rhs = jnp.concatenate(rhs, axis=1).astype(BF16)
+            both_k = lax.dot_general(
+                lhs, rhs, (((1,), (1,)), ((), ())), preferred_element_type=F32
             )
-            cols = []
-            for part in parts:
-                turned = pltpu.roll(part, lanes // 2, 1)
-                cols.append(
-                    jnp.concatenate(
-                        [
-                            jnp.where(low, part, none),
-                            jnp.where(low, turned, none),
-                            jnp.where(low, none, turned),
-                            jnp.where(low, none, part),
-                        ],
-                        axis=0,
-                    ).astype(BF16)
-                )
-            rhs = jnp.concatenate(cols, axis=1)
-            out[n % batch] = lax.dot_general(
-                lhs, rhs, (((1,), (1,)), ((), ())), preferred_element_type=F32
+            out[n % batch] = jnp.concatenate(
+                [both_k[:width], both_k[width:]], axis=1
             ).astype(BF16)
 
         passed[0] = mark[0]
@@ -274,7 +285,7 @@
         arrived.append(tuple(moved(planes[h], long[h], s) for h in range(2)))
     back = [[], []]
     token = bases[:1]
-    for s in range(ring):
+    for s in step_order(ring):
         *partial, token = contract(plan, s, rows, sibling, arrived[s], slot_pair, bases, token)
         for h in range(2):
             back[h].append(moved(partial[h], long[h], -s) if s else partial[h])

time: 234 us -> 207 us (0.88)
  the two profiles are of different devices: /device:TPU:24 before, /device:TPU:7 now
where the time goes in v2:
time: 207 us; the launch traced here: 205 us
  waiting for transfers between devices  74.7 us (36%)
  Pallas kernels  58.9 us (28%)
  starting transfers between devices  38.9 us (19%)
  blocking collectives  23.2 us (11%)
  local copies, waits for them, and re-layouts  4.47 us (2%)
  other arithmetic  3.8 us (2%)
    ppermute x25, waiting for transfers between devices, moved(): return lax.ppermute(value, axis, [(j, (j + step) % n) for j in range(n)])  61.6 us
    pallas_call x4, Pallas kernels, contract(): pl.pallas_call(kernel, grid_spec=pltpu.PrefetchScalarGridSpec(num_scalar_...  41.2 us
    ppermute x25, starting transfers between devices, moved(): return lax.ppermute(value, axis, [(j, (j + step) % n) for j in range(n)])  35.5 us
    all_to_all x1, blocking collectives, body(): lax.all_to_all(jnp.broadcast_to(mine, (nz, *mine.shape)), 'z', split_axis...  23.2 us
    all_to_all x1, waiting for transfers between devices, body(): line = lax.all_to_all(line, 'z', split_axis=0, concat_axis=0, tiled=True)  13 us
    pallas_call x1, Pallas kernels, collect(): pl.pallas_call(kernel, grid_spec=pltpu.PrefetchScalarGridSpec(num_scalar_...  12.6 us
  transfers between devices with their start and end apart: 26, of which 11 were waited for; matrix products, arithmetic and copies ran while one was open for 2% of the time, Pallas kernels for 16%

profile of v2, /device:TPU:7, one launch (start us, length us, event | category | flops | bytes accessed | tf_op | source)
XLA Modules:
  0.0 205.1 jit_solution(7287576390602845539)
XLA Ops:
  0.7 0.5 fusion.15.base.base_of
  1.2 12.6 %collect.1 = bf16[384,64,128]{2,1,0:T(8,128)(2,1)} custom-call(s32[768]{0:T(1024)} %sp.9, s32[64]{0:T(128)} %fusion.15.base.base_of, bf16[768,64,128]{2,1,0:T(8,128)(2,1)} %bitcast.56, bf16[768,64,128]{2,1,0:T(8,128)(2,1)} %bitcast.34, bf16[768,64,128]{2,1,0:T(8,128)(2,1)} %bitcast.35, bf16[768,64,128]{2,1,0:T(8,128)(2,1)} %bitcast.36, ...), custom_call_target="tpu_custom_call" | custom-call | flops 384000000 | bytes 12582912 | tf_op jit(solution)/shard_map/collect/pallas_call | solution.py:65
  13.8 0.8 collective-permute-start
  14.9 0.6 copy-done.3
  15.8 23.2 %all_to_all.10 = bf16[8,3,64,128]{3,2,1,0:T(8,128)(2,1)S(1)} all-to-all(bf16[8,3,64,128]{3,2,1,0:T(8,128)(2,1)S(1)} %broadcast_in_dim.12), channel_id=1, replica_groups=mesh['z'=8,'y'=4,'x'=4,'core'=2] {'z'}, dimensions={0} | all-to-all | bytes 786432 | tf_op jit(solution)/shard_map/all_to_all | solution.py:271
  39.3 2.1 %collective-permute-start.2 = (bf16[12,64,128]{2,1,0:T(8,128)(2,1)S(1)}, bf16[12,64,128]{2,1,0:T(8,128)(2,1)S(1)}, u32[]{:S(2)}, u32[]{:S(2)}) collective-permute-start(bf16[12,64,128]{2,1,0:T(8,128)(2,1)S(1)} %bitcast.158), channel_id=1, source_target_pairs={{0,4},{2,6},{4,0},{6,2},{1,5},{3,7},{5,1},{7,3},{8,12},{10,14},{12... | collective-permute-start | bytes 589832 | tf_op jit(solution)/shard_map/ppermute | solution.py:16
  41.4 1.3 collective-permute-start.4
  42.7 2.4 %collective-permute-done.1.refs_0_ = bf16[12,64,128]{2,1,0:T(8,128)(2,1)S(1)} collective-permute-done((bf16[12,64,128]{2,1,0:T(8,128)(2,1)S(1)}, bf16[12,64,128]{2,1,0:T(8,128)(2,1)S(1)}, u32[]{:S(2)}, u32[]{:S(2)}) %collective-permute-start.1) | collective-permute-done | bytes 196640 | tf_op jit(solution)/shard_map/ppermute | solution.py:16
  45.1 2.9 %collective-permute-start.5 = (bf16[12,64,128]{2,1,0:T(8,128)(2,1)S(1)}, bf16[12,64,128]{2,1,0:T(8,128)(2,1)S(1)}, u32[]{:S(2)}, u32[]{:S(2)}) collective-permute-start(bf16[12,64,128]{2,1,0:T(8,128)(2,1)S(1)} %bitcast.155), channel_id=1, source_target_pairs={{0,16},{8,24},{16,0},{24,8},{1,17},{9,25},{17,1},{25,9},{2,18},{10... | collective-permute-start | bytes 589832 | tf_op jit(solution)/shard_map/ppermute | solution.py:16
  48.0 1.2 collective-permute-start.6
  49.3 2.5 %collective-permute-done.3.refs_2_ = bf16[12,64,128]{2,1,0:T(8,128)(2,1)S(1)} collective-permute-done((bf16[12,64,128]{2,1,0:T(8,128)(2,1)S(1)}, bf16[12,64,128]{2,1,0:T(8,128)(2,1)S(1)}, u32[]{:S(2)}, u32[]{:S(2)}) %collective-permute-start.3) | collective-permute-done | bytes 196640 | tf_op jit(solution)/shard_map/ppermute | solution.py:16
  51.8 1.8 collective-permute-done.5.refs_4_
  53.6 1.9 collective-permute-done.6.refs_5_
  55.5 0.6 copy-done.14
  56.2 2.6 %assemble.1 = (bf16[48,64,128]{2,1,0:T(8,128)(2,1)}, bf16[48,64,128]{2,1,0:T(8,128)(2,1)}) custom-call(bf16[24,64,128]{2,1,0:T(8,128)(2,1)} %bitcast.153, bf16[12,64,128]{2,1,0:T(8,128)(2,1)} %copy-done.9, bf16[12,64,128]{2,1,0:T(8,128)(2,1)} %copy-done.10, bf16[12,64,128]{2,1,0:T(8,128)(2,1)} %copy-done.11, bf16[12,64,128]{2,1,0:T(8,128)(2,1)} %copy-done.12, ...), custom_call_target="tpu_custom_call" | custom-call | tf_op jit(solution)/shard_map/assemble/pallas_call | solution.py:95
  58.8 2.6 %collective-permute-start.7 = (bf16[48,64,128]{2,1,0:T(8,128)(2,1)}, bf16[48,64,128]{2,1,0:T(8,128)(2,1)S(1)}, u32[]{:S(2)}, u32[]{:S(2)}) collective-permute-start(bf16[48,64,128]{2,1,0:T(8,128)(2,1)} %get-tuple-element.17.refs_25_), channel_id=1, source_target_pairs={{0,8},{8,16},{16,24},{24,0},{1,9},{9,17},{17,25},{25,1},{2,10},{10... | collective-permute-start | bytes 2359304 | tf_op jit(solution)/shard_map/ppermute | solution.py:16
  61.4 1.1 collective-permute-start.8
  62.5 2.1 %collective-permute-start.10 = (bf16[48,64,128]{2,1,0:T(8,128)(2,1)}, bf16[48,64,128]{2,1,0:T(8,128)(2,1)}, u32[]{:S(2)}, u32[]{:S(2)}) collective-permute-start(bf16[48,64,128]{2,1,0:T(8,128)(2,1)} %get-tuple-element.17.refs_25_), channel_id=1, source_target_pairs={{0,24},{8,0},{16,8},{24,16},{1,25},{9,1},{17,9},{25,17},{2,26},{10... | collective-permute-start | bytes 2359304 | tf_op jit(solution)/shard_map/ppermute | solution.py:16
  64.7 13.5 %collective-permute-done.7.refs_25_ = bf16[48,64,128]{2,1,0:T(8,128)(2,1)S(1)} collective-permute-done((bf16[48,64,128]{2,1,0:T(8,128)(2,1)}, bf16[48,64,128]{2,1,0:T(8,128)(2,1)S(1)}, u32[]{:S(2)}, u32[]{:S(2)}) %collective-permute-start.7) | collective-permute-done | bytes 786464 | tf_op jit(solution)/shard_map/ppermute | solution.py:16
  78.2 1.2 collective-permute-start.13
  79.9 10.2 %contract.4 = (bf16[48,64,128]{2,1,0:T(8,128)(2,1)}, bf16[48,64,128]{2,1,0:T(8,128)(2,1)}, s32[1]{0:T(128)}) custom-call(s32[768]{0:T(1024)} %sp.9, s32[64]{0:T(128)} %fusion.15.base.base_of, s32[1]{0:T(128)} %bitcast.161, bf16[768,64,128]{2,1,0:T(8,128)(2,1)} %bitcast.57, bf16[768,64,128]{2,1,0:T(8,128)(2,1)} %bitcast.58, bf16[768,64,128]{2,1,0:T(8,128)(2,1)} %bitcast.59, ...), custom_call_target="tpu_custom_call" | custom-call | flops 1610612736 | bytes 6291456 | tf_op jit(solution)/shard_map/contract/pallas_call | solution.py:174
  90.1 0.9 copy-done.6
  91.0 10.2 %contract.5 = (bf16[48,64,128]{2,1,0:T(8,128)(2,1)}, bf16[48,64,128]{2,1,0:T(8,128)(2,1)}, s32[1]{0:T(128)}) custom-call(s32[768]{0:T(1024)} %sp.9, s32[64]{0:T(128)} %fusion.15.base.base_of, s32[1]{0:T(128)} %get-tuple-element.20.mark, bf16[768,64,128]{2,1,0:T(8,128)(2,1)} %bitcast.92, bf16[768,64,128]{2,1,0:T(8,128)(2,1)} %bitcast.82, ...), custom_call_target="tpu_custom_call" | custom-call | flops 1610612736 | bytes 6291456 | tf_op jit(solution)/shard_map/contract/pallas_call | solution.py:174
  101.3 10.3 %contract.6 = (bf16[48,64,128]{2,1,0:T(8,128)(2,1)}, bf16[48,64,128]{2,1,0:T(8,128)(2,1)}, s32[1]{0:T(128)}) custom-call(s32[768]{0:T(1024)} %sp.9, s32[64]{0:T(128)} %fusion.15.base.base_of, s32[1]{0:T(128)} %get-tuple-element.22.mark, bf16[768,64,128]{2,1,0:T(8,128)(2,1)} %bitcast.117, bf16[768,64,128]{2,1,0:T(8,128)(2,1)} %bitcast.106, ...), custom_call_target="tpu_custom_call" | custom-call | flops 1610612736 | bytes 6291456 | tf_op jit(solution)/shard_map/contract/pallas_call | solution.py:174
  111.6 10.5 %contract.7 = (bf16[48,64,128]{2,1,0:T(8,128)(2,1)}, bf16[48,64,128]{2,1,0:T(8,128)(2,1)}, s32[1]{0:T(128)}) custom-call(s32[768]{0:T(1024)} %sp.9, s32[64]{0:T(128)} %fusion.15.base.base_of, s32[1]{0:T(128)} %get-tuple-element.24.mark, bf16[768,64,128]{2,1,0:T(8,128)(2,1)} %bitcast.129, bf16[768,64,128]{2,1,0:T(8,128)(2,1)} %bitcast.130, ...), custom_call_target="tpu_custom_call" | custom-call | flops 1610612736 | bytes 6291456 | tf_op jit(solution)/shard_map/contract/pallas_call | solution.py:174
  122.1 2.6 %collective-permute-start.21 = (bf16[48,64,128]{2,1,0:T(8,128)(2,1)}, bf16[48,64,128]{2,1,0:T(8,128)(2,1)S(1)}, u32[]{:S(2)}, u32[]{:S(2)}) collective-permute-start(bf16[48,64,128]{2,1,0:T(8,128)(2,1)} %get-tuple-element.29), channel_id=1, source_target_pairs={{0,4},{2,6},{4,0},{6,2},{1,5},{3,7},{5,1},{7,3},{8,12},{10,14},{12... | collective-permute-start | bytes 2359304 | tf_op jit(solution)/shard_map/ppermute | solution.py:16
  124.7 1.8 collective-permute-start.20
  127.0 2.7 %collective-permute-start.15 = (bf16[48,64,128]{2,1,0:T(8,128)(2,1)}, bf16[48,64,128]{2,1,0:T(8,128)(2,1)S(1)}, u32[]{:S(2)}, u32[]{:S(2)}) collective-permute-start(bf16[48,64,128]{2,1,0:T(8,128)(2,1)} %get-tuple-element.25), channel_id=1, source_target_pairs={{0,16},{8,24},{16,0},{24,8},{1,17},{9,25},{17,1},{25,9},{2,18},{10... | collective-permute-start | bytes 2359304 | tf_op jit(solution)/shard_map/ppermute | solution.py:16
  129.8 9.9 %collective-permute-done.21 = bf16[48,64,128]{2,1,0:T(8,128)(2,1)S(1)} collective-permute-done((bf16[48,64,128]{2,1,0:T(8,128)(2,1)}, bf16[48,64,128]{2,1,0:T(8,128)(2,1)S(1)}, u32[]{:S(2)}, u32[]{:S(2)}) %collective-permute-start.21) | collective-permute-done | bytes 786464 | tf_op jit(solution)/shard_map/ppermute | solution.py:16
  139.7 2.6 %collective-permute-start.9 = (bf16[48,64,128]{2,1,0:T(8,128)(2,1)S(1)}, bf16[48,64,128]{2,1,0:T(8,128)(2,1)S(1)}, u32[]{:S(2)}, u32[]{:S(2)}) collective-permute-start(bf16[48,64,128]{2,1,0:T(8,128)(2,1)S(1)} %copy-done.19), channel_id=1, source_target_pairs={{0,24},{8,0},{16,8},{24,16},{1,25},{9,1},{17,9},{25,17},{2,26},{10... | collective-permute-start | bytes 2359304 | tf_op jit(solution)/shard_map/ppermute | solution.py:16
  142.3 18.4 %collective-permute-done.20 = bf16[48,64,128]{2,1,0:T(8,128)(2,1)S(1)} collective-permute-done((bf16[48,64,128]{2,1,0:T(8,128)(2,1)}, bf16[48,64,128]{2,1,0:T(8,128)(2,1)S(1)}, u32[]{:S(2)}, u32[]{:S(2)}) %collective-permute-start.20) | collective-permute-done | bytes 786464 | tf_op jit(solution)/shard_map/ppermute | solution.py:16
  160.8 0.6 add_convert_fusion
  161.4 1.7 collective-permute-start.24
  163.1 1.8 collective-permute-start.23
  164.9 1.4 collective-permute-start.22
  166.3 0.6 add_convert_fusion.1
  167.0 3.4 %collective-permute-start.18 = (bf16[12,64,128]{2,1,0:T(8,128)(2,1)S(1)}, bf16[12,64,128]{2,1,0:T(8,128)(2,1)S(1)}, u32[]{:S(2)}, u32[]{:S(2)}) collective-permute-start(bf16[12,64,128]{2,1,0:T(8,128)(2,1)S(1)} %get-tuple-element.33), channel_id=1, source_target_pairs={{0,2},{2,4},{4,6},{6,0},{1,3},{3,5},{5,7},{7,1},{8,10},{10,12},{12... | collective-permute-start | bytes 589832 | tf_op jit(solution)/shard_map/ppermute | solution.py:16
  170.4 0.7 collective-permute-start.16
  171.0 0.9 collective-permute-done.23
  172.1 6.2 %collective-permute-done.18 = bf16[12,64,128]{2,1,0:T(8,128)(2,1)S(1)} collective-permute-done((bf16[12,64,128]{2,1,0:T(8,128)(2,1)S(1)}, bf16[12,64,128]{2,1,0:T(8,128)(2,1)S(1)}, u32[]{:S(2)}, u32[]{:S(2)}) %collective-permute-start.18) | collective-permute-done | bytes 196640 | tf_op jit(solution)/shard_map/ppermute | solution.py:16
  178.3 4.2 %collective-permute-done.16 = bf16[12,64,128]{2,1,0:T(8,128)(2,1)S(1)} collective-permute-done((bf16[12,64,128]{2,1,0:T(8,128)(2,1)S(1)}, bf16[12,64,128]{2,1,0:T(8,128)(2,1)S(1)}, u32[]{:S(2)}, u32[]{:S(2)}) %collective-permute-start.16) | collective-permute-done | bytes 196640 | tf_op jit(solution)/shard_map/ppermute | solution.py:16
  182.6 0.8 pad_maximum_fusion
  183.4 3.5 %all-to-all-start.1 = ((bf16[8,3,64,128]{3,2,1,0:T(8,128)(2,1)}), bf16[8,3,64,128]{3,2,1,0:T(8,128)(2,1)S(1)}, u32[]{:S(2)}, u32[]{:S(2)}) async-start(bf16[8,3,64,128]{3,2,1,0:T(8,128)(2,1)} %bitcast.9), calls=%async_computation.1 | async-start | bytes 786432 | tf_op jit(solution)/shard_map/all_to_all | solution.py:298
  187.0 0.7 mul.56.sq_ref
  188.2 0.7 broadcast_subtract_fusion.den_ref
  188.9 13.0 %all-to-all-done.1.line_ref = bf16[8,3,64,128]{3,2,1,0:T(8,128)(2,1)S(1)} async-done(((bf16[8,3,64,128]{3,2,1,0:T(8,128)(2,1)}), bf16[8,3,64,128]{3,2,1,0:T(8,128)(2,1)S(1)}, u32[]{:S(2)}, u32[]{:S(2)}) %all-to-all-start.1) | async-done | bytes 393248 | tf_op jit(solution)/shard_map/all_to_all | solution.py:298
  201.9 0.8 copy-done.2
  202.7 2.5 %finish.1 = (f32[3,64,128]{2,1,0:T(8,128)}, bf16[3,64,128]{2,1,0:T(8,128)(2,1)}) custom-call(bf16[8,3,64,128]{3,2,1,0:T(8,128)(2,1)} %copy-done.2, bf16[3,64,128]{2,1,0:T(8,128)(2,1)} %bitcast.160, f32[3,32,128]{2,1,0:T(8,128)} %broadcast_subtract_fusion.den_ref, f32[3,32,128]{2,1,0:T(8,128)} %mul.56.sq_ref), custom_call_target="tpu_custom_call" | custom-call | tf_op jit(solution)/shard_map/finish/pallas_call | solution.py:232
  (80 shorter events, 3.1 us)
Async XLA Ops:
  0.6 187.2 %copy-start = (f32[48]{0:T(128)S(1)}, f32[48]{0:T(128)}, u32[]{:S(2)}) copy-start(f32[48]{0:T(128)} %param.13) | copy-start | bytes 580
  1.2 13.4 %copy-start.15 = (bf16[3,2,4096]{2,1,0:T(2,128)(2,1)S(1)}, bf16[3,2,4096]{2,1,0:T(2,128)(2,1)}, u32[]{:S(2)}) copy-start(bf16[3,2,4096]{2,1,0:T(2,128)(2,1)} %param.9) | copy-start | bytes 147460
  1.2 13.5 %copy-start.18 = (s32[3]{0:T(128)S(1)}, s32[3]{0:T(128)}, u32[]{:S(2)}) copy-start(s32[3]{0:T(128)} %param.10) | copy-start | bytes 40
  13.8 65.6 %collective-permute-start = (bf16[384,64,128]{2,1,0:T(8,128)(2,1)}, bf16[384,64,128]{2,1,0:T(8,128)(2,1)}, u32[]{:S(2)}, u32[]{:S(2)}) collective-permute-start(bf16[384,64,128]{2,1,0:T(8,128)(2,1)} %collect.1), channel_id=1, source_target_pairs={{0,1},{1,0},{2,3},{3,2},{4,5},{5,4},{6,7},{7,6},{8,9},{9,8},{10,11... | collective-permute-start | bytes 18874376 | tf_op jit(solution)/shard_map/ppermute | solution.py:16
  14.9 0.6 copy-start.3
  39.0 16.5 %copy-start.1 = (bf16[8,3,64,128]{3,2,1,0:T(8,128)(2,1)}, bf16[8,3,64,128]{3,2,1,0:T(8,128)(2,1)S(1)}, u32[]{:S(2)}) copy-start(bf16[8,3,64,128]{3,2,1,0:T(8,128)(2,1)S(1)} %all_to_all.10) | copy-start | bytes 1179652
  39.0 6.1 %collective-permute-start.1 = (bf16[12,64,128]{2,1,0:T(8,128)(2,1)S(1)}, bf16[12,64,128]{2,1,0:T(8,128)(2,1)S(1)}, u32[]{:S(2)}, u32[]{:S(2)}) collective-permute-start(bf16[12,64,128]{2,1,0:T(8,128)(2,1)S(1)} %bitcast.157), channel_id=1, source_target_pairs={{0,2},{2,4},{4,6},{6,0},{1,3},{3,5},{5,7},{7,1},{8,10},{10,12},{12... | collective-permute-start | bytes 589832 | tf_op jit(solution)/shard_map/ppermute | solution.py:16
  39.3 8.7 %collective-permute-start.2 = (bf16[12,64,128]{2,1,0:T(8,128)(2,1)S(1)}, bf16[12,64,128]{2,1,0:T(8,128)(2,1)S(1)}, u32[]{:S(2)}, u32[]{:S(2)}) collective-permute-start(bf16[12,64,128]{2,1,0:T(8,128)(2,1)S(1)} %bitcast.158), channel_id=1, source_target_pairs={{0,4},{2,6},{4,0},{6,2},{1,5},{3,7},{5,1},{7,3},{8,12},{10,14},{12... | collective-permute-start | bytes 589832 | tf_op jit(solution)/shard_map/ppermute | solution.py:16
  41.4 10.3 %collective-permute-start.3 = (bf16[12,64,128]{2,1,0:T(8,128)(2,1)S(1)}, bf16[12,64,128]{2,1,0:T(8,128)(2,1)S(1)}, u32[]{:S(2)}, u32[]{:S(2)}) collective-permute-start(bf16[12,64,128]{2,1,0:T(8,128)(2,1)S(1)} %bitcast.159), channel_id=1, source_target_pairs={{0,6},{2,0},{4,2},{6,4},{1,7},{3,1},{5,3},{7,5},{8,14},{10,8},{12,... | collective-permute-start | bytes 589832 | tf_op jit(solution)/shard_map/ppermute | solution.py:16
  41.4 10.3 %collective-permute-start.4 = (bf16[12,64,128]{2,1,0:T(8,128)(2,1)S(1)}, bf16[12,64,128]{2,1,0:T(8,128)(2,1)S(1)}, u32[]{:S(2)}, u32[]{:S(2)}) collective-permute-start(bf16[12,64,128]{2,1,0:T(8,128)(2,1)S(1)} %bitcast.154), channel_id=1, source_target_pairs={{0,8},{8,16},{16,24},{24,0},{1,9},{9,17},{17,25},{25,1},{2,10},{10... | collective-permute-start | bytes 589832 | tf_op jit(solution)/shard_map/ppermute | solution.py:16
  45.1 10.4 %copy-start.9 = (bf16[12,64,128]{2,1,0:T(8,128)(2,1)}, bf16[12,64,128]{2,1,0:T(8,128)(2,1)S(1)}, u32[]{:S(2)}) copy-start(bf16[12,64,128]{2,1,0:T(8,128)(2,1)S(1)} %collective-permute-done.1.refs_0_) | copy-start | bytes 589828
  45.1 8.4 %collective-permute-start.5 = (bf16[12,64,128]{2,1,0:T(8,128)(2,1)S(1)}, bf16[12,64,128]{2,1,0:T(8,128)(2,1)S(1)}, u32[]{:S(2)}, u32[]{:S(2)}) collective-permute-start(bf16[12,64,128]{2,1,0:T(8,128)(2,1)S(1)} %bitcast.155), channel_id=1, source_target_pairs={{0,16},{8,24},{16,0},{24,8},{1,17},{9,25},{17,1},{25,9},{2,18},{10... | collective-permute-start | bytes 589832 | tf_op jit(solution)/shard_map/ppermute | solution.py:16
  48.0 7.5 %copy-start.10 = (bf16[12,64,128]{2,1,0:T(8,128)(2,1)}, bf16[12,64,128]{2,1,0:T(8,128)(2,1)S(1)}, u32[]{:S(2)}) copy-start(bf16[12,64,128]{2,1,0:T(8,128)(2,1)S(1)} %collective-permute-done.2.refs_1_) | copy-start | bytes 589828
  48.0 7.5 %collective-permute-start.6 = (bf16[12,64,128]{2,1,0:T(8,128)(2,1)S(1)}, bf16[12,64,128]{2,1,0:T(8,128)(2,1)S(1)}, u32[]{:S(2)}, u32[]{:S(2)}) collective-permute-start(bf16[12,64,128]{2,1,0:T(8,128)(2,1)S(1)} %bitcast.156), channel_id=1, source_target_pairs={{0,24},{8,0},{16,8},{24,16},{1,25},{9,1},{17,9},{25,17},{2,26},{10... | collective-permute-start | bytes 589832 | tf_op jit(solution)/shard_map/ppermute | solution.py:16
  51.8 3.7 %copy-start.11 = (bf16[12,64,128]{2,1,0:T(8,128)(2,1)}, bf16[12,64,128]{2,1,0:T(8,128)(2,1)S(1)}, u32[]{:S(2)}) copy-start(bf16[12,64,128]{2,1,0:T(8,128)(2,1)S(1)} %collective-permute-done.3.refs_2_) | copy-start | bytes 589828
  51.8 3.7 %copy-start.12 = (bf16[12,64,128]{2,1,0:T(8,128)(2,1)}, bf16[12,64,128]{2,1,0:T(8,128)(2,1)S(1)}, u32[]{:S(2)}) copy-start(bf16[12,64,128]{2,1,0:T(8,128)(2,1)S(1)} %collective-permute-done.4.refs_3_) | copy-start | bytes 589828
  53.6 2.0 copy-start.13
  55.5 0.7 copy-start.14
  58.8 19.4 %collective-permute-start.7 = (bf16[48,64,128]{2,1,0:T(8,128)(2,1)}, bf16[48,64,128]{2,1,0:T(8,128)(2,1)S(1)}, u32[]{:S(2)}, u32[]{:S(2)}) collective-permute-start(bf16[48,64,128]{2,1,0:T(8,128)(2,1)} %get-tuple-element.17.refs_25_), channel_id=1, source_target_pairs={{0,8},{8,16},{16,24},{24,0},{1,9},{9,17},{17,25},{25,1},{2,10},{10... | collective-permute-start | bytes 2359304 | tf_op jit(solution)/shard_map/ppermute | solution.py:16
  61.4 28.8 %collective-permute-start.8 = (bf16[48,64,128]{2,1,0:T(8,128)(2,1)}, bf16[48,64,128]{2,1,0:T(8,128)(2,1)S(1)}, u32[]{:S(2)}, u32[]{:S(2)}) collective-permute-start(bf16[48,64,128]{2,1,0:T(8,128)(2,1)} %get-tuple-element.18.refs_26_), channel_id=1, source_target_pairs={{0,2},{2,4},{4,6},{6,0},{1,3},{3,5},{5,7},{7,1},{8,10},{10,12},{12... | collective-permute-start | bytes 2359304 | tf_op jit(solution)/shard_map/ppermute | solution.py:16
  62.5 38.7 %collective-permute-start.10 = (bf16[48,64,128]{2,1,0:T(8,128)(2,1)}, bf16[48,64,128]{2,1,0:T(8,128)(2,1)}, u32[]{:S(2)}, u32[]{:S(2)}) collective-permute-start(bf16[48,64,128]{2,1,0:T(8,128)(2,1)} %get-tuple-element.17.refs_25_), channel_id=1, source_target_pairs={{0,24},{8,0},{16,8},{24,16},{1,25},{9,1},{17,9},{25,17},{2,26},{10... | collective-permute-start | bytes 2359304 | tf_op jit(solution)/shard_map/ppermute | solution.py:16
  64.6 36.7 %collective-permute-start.11 = (bf16[48,64,128]{2,1,0:T(8,128)(2,1)}, bf16[48,64,128]{2,1,0:T(8,128)(2,1)}, u32[]{:S(2)}, u32[]{:S(2)}) collective-permute-start(bf16[48,64,128]{2,1,0:T(8,128)(2,1)} %get-tuple-element.18.refs_26_), channel_id=1, source_target_pairs={{0,6},{2,0},{4,2},{6,4},{1,7},{3,1},{5,3},{7,5},{8,14},{10,8},{12,... | collective-permute-start | bytes 2359304 | tf_op jit(solution)/shard_map/ppermute | solution.py:16
  78.2 11.9 %copy-start.5 = (bf16[48,64,128]{2,1,0:T(8,128)(2,1)}, bf16[48,64,128]{2,1,0:T(8,128)(2,1)S(1)}, u32[]{:S(2)}) copy-start(bf16[48,64,128]{2,1,0:T(8,128)(2,1)S(1)} %collective-permute-done.7.refs_25_) | copy-start | bytes 2359300
  78.2 33.3 %collective-permute-start.13 = (bf16[48,64,128]{2,1,0:T(8,128)(2,1)}, bf16[48,64,128]{2,1,0:T(8,128)(2,1)}, u32[]{:S(2)}, u32[]{:S(2)}) collective-permute-start(bf16[48,64,128]{2,1,0:T(8,128)(2,1)} %get-tuple-element.17.refs_25_), channel_id=1, source_target_pairs={{0,16},{8,24},{16,0},{24,8},{1,17},{9,25},{17,1},{25,9},{2,18},{10... | collective-permute-start | bytes 2359304 | tf_op jit(solution)/shard_map/ppermute | solution.py:16
  79.4 32.1 %collective-permute-start.14 = (bf16[48,64,128]{2,1,0:T(8,128)(2,1)}, bf16[48,64,128]{2,1,0:T(8,128)(2,1)}, u32[]{:S(2)}, u32[]{:S(2)}) collective-permute-start(bf16[48,64,128]{2,1,0:T(8,128)(2,1)} %get-tuple-element.18.refs_26_), channel_id=1, source_target_pairs={{0,4},{2,6},{4,0},{6,2},{1,5},{3,7},{5,1},{7,3},{8,12},{10,14},{12... | collective-permute-start | bytes 2359304 | tf_op jit(solution)/shard_map/ppermute | solution.py:16
  90.1 0.9 copy-start.6
  111.6 15.0 %copy-start.21 = (bf16[48,64,128]{2,1,0:T(8,128)(2,1)S(1)}, bf16[48,64,128]{2,1,0:T(8,128)(2,1)}, u32[]{:S(2)}) copy-start(bf16[48,64,128]{2,1,0:T(8,128)(2,1)} %get-tuple-element.27) | copy-start | bytes 2359300
  111.6 18.2 %copy-start.20 = (bf16[48,64,128]{2,1,0:T(8,128)(2,1)S(1)}, bf16[48,64,128]{2,1,0:T(8,128)(2,1)}, u32[]{:S(2)}) copy-start(bf16[48,64,128]{2,1,0:T(8,128)(2,1)} %get-tuple-element.23) | copy-start | bytes 2359300
  111.6 28.1 %copy-start.19 = (bf16[48,64,128]{2,1,0:T(8,128)(2,1)S(1)}, bf16[48,64,128]{2,1,0:T(8,128)(2,1)}, u32[]{:S(2)}) copy-start(bf16[48,64,128]{2,1,0:T(8,128)(2,1)} %get-tuple-element.21) | copy-start | bytes 2359300
  111.6 49.2 %copy-start.8 = (bf16[48,64,128]{2,1,0:T(8,128)(2,1)S(1)}, bf16[48,64,128]{2,1,0:T(8,128)(2,1)}, u32[]{:S(2)}) copy-start(bf16[48,64,128]{2,1,0:T(8,128)(2,1)} %get-tuple-element.26) | copy-start | bytes 2359300
  122.1 17.6 %collective-permute-start.21 = (bf16[48,64,128]{2,1,0:T(8,128)(2,1)}, bf16[48,64,128]{2,1,0:T(8,128)(2,1)S(1)}, u32[]{:S(2)}, u32[]{:S(2)}) collective-permute-start(bf16[48,64,128]{2,1,0:T(8,128)(2,1)} %get-tuple-element.29), channel_id=1, source_target_pairs={{0,4},{2,6},{4,0},{6,2},{1,5},{3,7},{5,1},{7,3},{8,12},{10,14},{12... | collective-permute-start | bytes 2359304 | tf_op jit(solution)/shard_map/ppermute | solution.py:16
  124.7 36.0 %collective-permute-start.20 = (bf16[48,64,128]{2,1,0:T(8,128)(2,1)}, bf16[48,64,128]{2,1,0:T(8,128)(2,1)S(1)}, u32[]{:S(2)}, u32[]{:S(2)}) collective-permute-start(bf16[48,64,128]{2,1,0:T(8,128)(2,1)} %get-tuple-element.28), channel_id=1, source_target_pairs={{0,2},{2,4},{4,6},{6,0},{1,3},{3,5},{5,7},{7,1},{8,10},{10,12},{12... | collective-permute-start | bytes 2359304 | tf_op jit(solution)/shard_map/ppermute | solution.py:16
  126.5 34.2 %collective-permute-start.19 = (bf16[48,64,128]{2,1,0:T(8,128)(2,1)S(1)}, bf16[48,64,128]{2,1,0:T(8,128)(2,1)S(1)}, u32[]{:S(2)}, u32[]{:S(2)}) collective-permute-start(bf16[48,64,128]{2,1,0:T(8,128)(2,1)S(1)} %copy-done.21), channel_id=1, source_target_pairs={{0,6},{2,0},{4,2},{6,4},{1,7},{3,1},{5,3},{7,5},{8,14},{10,8},{12,... | collective-permute-start | bytes 2359304 | tf_op jit(solution)/shard_map/ppermute | solution.py:16
  127.0 37.9 %collective-permute-start.15 = (bf16[48,64,128]{2,1,0:T(8,128)(2,1)}, bf16[48,64,128]{2,1,0:T(8,128)(2,1)S(1)}, u32[]{:S(2)}, u32[]{:S(2)}) collective-permute-start(bf16[48,64,128]{2,1,0:T(8,128)(2,1)} %get-tuple-element.25), channel_id=1, source_target_pairs={{0,16},{8,24},{16,0},{24,8},{1,17},{9,25},{17,1},{25,9},{2,18},{10... | collective-permute-start | bytes 2359304 | tf_op jit(solution)/shard_map/ppermute | solution.py:16
  129.7 36.6 %collective-permute-start.12 = (bf16[48,64,128]{2,1,0:T(8,128)(2,1)S(1)}, bf16[48,64,128]{2,1,0:T(8,128)(2,1)S(1)}, u32[]{:S(2)}, u32[]{:S(2)}) collective-permute-start(bf16[48,64,128]{2,1,0:T(8,128)(2,1)S(1)} %copy-done.20), channel_id=1, source_target_pairs={{0,8},{8,16},{16,24},{24,0},{1,9},{9,17},{17,25},{25,1},{2,10},{10... | collective-permute-start | bytes 2359304 | tf_op jit(solution)/shard_map/ppermute | solution.py:16
  139.7 26.6 %collective-permute-start.9 = (bf16[48,64,128]{2,1,0:T(8,128)(2,1)S(1)}, bf16[48,64,128]{2,1,0:T(8,128)(2,1)S(1)}, u32[]{:S(2)}, u32[]{:S(2)}) collective-permute-start(bf16[48,64,128]{2,1,0:T(8,128)(2,1)S(1)} %copy-done.19), channel_id=1, source_target_pairs={{0,24},{8,0},{16,8},{24,16},{1,25},{9,1},{17,9},{25,17},{2,26},{10... | collective-permute-start | bytes 2359304 | tf_op jit(solution)/shard_map/ppermute | solution.py:16
  161.4 4.9 %copy-start.7 = (bf16[48,64,128]{2,1,0:T(8,128)(2,1)S(1)}, bf16[48,64,128]{2,1,0:T(8,128)(2,1)}, u32[]{:S(2)}) copy-start(bf16[48,64,128]{2,1,0:T(8,128)(2,1)} %get-tuple-element.19) | copy-start | bytes 2359300
  161.4 8.9 %collective-permute-start.24 = (bf16[12,64,128]{2,1,0:T(8,128)(2,1)S(1)}, bf16[12,64,128]{2,1,0:T(8,128)(2,1)S(1)}, u32[]{:S(2)}, u32[]{:S(2)}) collective-permute-start(bf16[12,64,128]{2,1,0:T(8,128)(2,1)S(1)} %get-tuple-element.36), channel_id=1, source_target_pairs={{0,8},{8,16},{16,24},{24,0},{1,9},{9,17},{17,25},{25,1},{2,10},{10... | collective-permute-start | bytes 589832 | tf_op jit(solution)/shard_map/ppermute | solution.py:16
  163.1 8.9 %collective-permute-start.23 = (bf16[12,64,128]{2,1,0:T(8,128)(2,1)S(1)}, bf16[12,64,128]{2,1,0:T(8,128)(2,1)S(1)}, u32[]{:S(2)}, u32[]{:S(2)}) collective-permute-start(bf16[12,64,128]{2,1,0:T(8,128)(2,1)S(1)} %get-tuple-element.37), channel_id=1, source_target_pairs={{0,16},{8,24},{16,0},{24,8},{1,17},{9,25},{17,1},{25,9},{2,18},{10... | collective-permute-start | bytes 589832 | tf_op jit(solution)/shard_map/ppermute | solution.py:16
  164.9 7.0 %collective-permute-start.22 = (bf16[12,64,128]{2,1,0:T(8,128)(2,1)S(1)}, bf16[12,64,128]{2,1,0:T(8,128)(2,1)S(1)}, u32[]{:S(2)}, u32[]{:S(2)}) collective-permute-start(bf16[12,64,128]{2,1,0:T(8,128)(2,1)S(1)} %get-tuple-element.35), channel_id=1, source_target_pairs={{0,24},{8,0},{16,8},{24,16},{1,25},{9,1},{17,9},{25,17},{2,26},{10... | collective-permute-start | bytes 589832 | tf_op jit(solution)/shard_map/ppermute | solution.py:16
  167.0 11.3 %collective-permute-start.18 = (bf16[12,64,128]{2,1,0:T(8,128)(2,1)S(1)}, bf16[12,64,128]{2,1,0:T(8,128)(2,1)S(1)}, u32[]{:S(2)}, u32[]{:S(2)}) collective-permute-start(bf16[12,64,128]{2,1,0:T(8,128)(2,1)S(1)} %get-tuple-element.33), channel_id=1, source_target_pairs={{0,2},{2,4},{4,6},{6,0},{1,3},{3,5},{5,7},{7,1},{8,10},{10,12},{12... | collective-permute-start | bytes 589832 | tf_op jit(solution)/shard_map/ppermute | solution.py:16
  170.4 7.9 %collective-permute-start.17 = (bf16[12,64,128]{2,1,0:T(8,128)(2,1)S(1)}, bf16[12,64,128]{2,1,0:T(8,128)(2,1)S(1)}, u32[]{:S(2)}, u32[]{:S(2)}) collective-permute-start(bf16[12,64,128]{2,1,0:T(8,128)(2,1)S(1)} %get-tuple-element.34), channel_id=1, source_target_pairs={{0,4},{2,6},{4,0},{6,2},{1,5},{3,7},{5,1},{7,3},{8,12},{10,14},{12... | collective-permute-start | bytes 589832 | tf_op jit(solution)/shard_map/ppermute | solution.py:16
  170.4 16.5 %copy-start.16 = (f32[3,64]{1,0:T(4,128)S(1)}, f32[3,64]{1,0:T(4,128)}, u32[]{:S(2)}) copy-start(f32[3,64]{1,0:T(4,128)} %param.12) | copy-start | bytes 2308
  170.4 12.1 %collective-permute-start.16 = (bf16[12,64,128]{2,1,0:T(8,128)(2,1)S(1)}, bf16[12,64,128]{2,1,0:T(8,128)(2,1)S(1)}, u32[]{:S(2)}, u32[]{:S(2)}) collective-permute-start(bf16[12,64,128]{2,1,0:T(8,128)(2,1)S(1)} %get-tuple-element.32), channel_id=1, source_target_pairs={{0,6},{2,0},{4,2},{6,4},{1,7},{3,1},{5,3},{7,5},{8,14},{10,8},{12,... | collective-permute-start | bytes 589832 | tf_op jit(solution)/shard_map/ppermute | solution.py:16
  172.1 14.9 %copy-start.4 = (f32[3,64,64]{2,1,0:T(8,128)S(1)}, f32[3,64,64]{2,1,0:T(8,128)}, u32[]{:S(2)}) copy-start(f32[3,64,64]{2,1,0:T(8,128)} %copy-done.3) | copy-start | bytes 147460
  172.1 15.6 %copy-start.17 = (s32[3,2]{0,1:T(2,128)S(1)}, s32[3,2]{0,1:T(2,128)}, u32[]{:S(2)}) copy-start(s32[3,2]{0,1:T(2,128)} %param.11) | copy-start | bytes 76
  183.4 18.5 %all-to-all-start.1 = ((bf16[8,3,64,128]{3,2,1,0:T(8,128)(2,1)}), bf16[8,3,64,128]{3,2,1,0:T(8,128)(2,1)S(1)}, u32[]{:S(2)}, u32[]{:S(2)}) async-start(bf16[8,3,64,128]{3,2,1,0:T(8,128)(2,1)} %bitcast.9), calls=%async_computation.1 | async-start | bytes 786432 | tf_op jit(solution)/shard_map/all_to_all | solution.py:298
  201.9 0.8 copy-start.2
